TPU v7x, 8 devices: a whole 2x2x1 slice. The times are simulated.
8 devices in a mesh: data: 8 (over z, y, x, core).
Axes of the slice: x: 2, y: 2, z: 1, core: 2. Of those that a mesh axis runs over, the one named last changes fastest.
Arguments:
- act_in: bfloat16 [8192, 896], P('data')
- pre_act: bfloat16 [8192, 4864], P('data')
- grad_out: bfloat16 [8192, 4864], P('data')
- q_init: float32 [4864, 8], replicated
- err_mem: float32 [8, 896, 4864], P('data')
Outputs:
- output 1: float32 [896, 8], replicated
- output 2: float32 [4864, 8], replicated
- output 3: float32 [8, 896, 4864], P('data')
All inputs are finite; a program needn't handle non-finite values.
Results may differ from a plain program's by a relative error of at most 0.001.
Values sent between devices are 32-bit elements.
A program may use at most 1 GiB of HBM per device.

v0:
```python
import jax
import jax.numpy as jnp
from jax import lax
from jax.sharding import PartitionSpec as P

EXACT_PREC = lax.Precision.HIGHEST


def gelu_grad(pre_act, grad_out):
    z_f32 = pre_act.astype(jnp.float32)
    _, pullback = jax.vjp(jax.nn.gelu, z_f32)
    return pullback(grad_out.astype(jnp.float32))[0]


def orthonormalize(p_sum):
    def gs_step(col_idx, ortho_cols):
        column = lax.dynamic_slice_in_dim(p_sum, col_idx, 1, axis=1)
        proj_coef = jnp.dot(column.T, ortho_cols, precision=EXACT_PREC)
        residual = column - jnp.dot(ortho_cols, proj_coef.T, precision=EXACT_PREC)
        unit_col = residual / jnp.sqrt(jnp.sum(residual * residual))
        return lax.dynamic_update_slice_in_dim(ortho_cols, unit_col, col_idx, axis=1)
    return lax.fori_loop(0, p_sum.shape[1], gs_step, jnp.zeros_like(p_sum))


def solution(mesh):
    group_size = mesh.shape['data']

    def per_device(act_in, pre_act, grad_out, q_init, err_mem):
        row_count = act_in.shape[0]
        grad_pre = gelu_grad(pre_act, grad_out).astype(jnp.bfloat16)
        grad_w = lax.dot_general(act_in, grad_pre, (((0,), (0,)), ((), ())), preferred_element_type=jnp.float32)
        merged = grad_w / row_count + err_mem[0]
        p_part = jnp.dot(merged, q_init, precision=EXACT_PREC)
        p_sum = lax.psum(p_part, 'data')
        p_factor = orthonormalize(p_sum)
        q_part = lax.dot_general(merged, p_factor, (((0,), (0,)), ((), ())), precision=EXACT_PREC)
        q_factor = lax.psum(q_part, 'data') / group_size
        approx = lax.dot_general(p_factor, q_factor, (((1,), (1,)), ((), ())), precision=EXACT_PREC)
        err_new = merged - approx
        return p_factor, q_factor, err_new[None]

    return jax.shard_map(per_device, mesh=mesh, in_specs=(P('data', None), P('data', None), P('data', None), P(None, None), P('data', None, None)), out_specs=(P(None, None), P(None, None), P('data', None, None)), check_vma=False)
```

profile of v0, /device:TPU:0, one launch (start us, length us, event | category | flops | bytes accessed | tf_op | source)
XLA Modules:
  0.0 224.1 jit_solution(9137830650714146707)
XLA Ops:
  7.2 19.0 %copy.8 = f32[1,896,4864]{1,2,0:T(8,128)} copy(f32[1,896,4864]{2,1,0:T(8,128)} %param.11) | data formatting | bytes 34865152 | tf_op args[4]
  26.2 33.3 %bitcast_add_fusion = f32[896,4864]{0,1:T(8,128)} fusion(f32[1,896,4864]{1,2,0:T(8,128)} %copy.8, bf16[1024,896]{1,0:T(8,128)(2,1)S(1)} %copy-done, bf16[1024,4864]{1,0:T(8,128)(2,1)} %param.9, bf16[1024,4864]{1,0:T(8,128)(2,1)} %param.8), kind=kOutput, calls=%fused_computation.22 | convolution fusion | flops 9043771392 | bytes 56623104 | tf_op jit(solution)/shard_map/dot_general | solution.py:31
  59.6 13.5 %fusion.25 = f32[896,8]{0,1:T(8,128)S(1)} fusion(f32[896,4864]{0,1:T(8,128)} %bitcast_add_fusion, f32[4864,8]{0,1:T(8,128)S(1)} %copy-done.4), kind=kOutput, calls=%fused_computation.36 | convolution fusion | flops 418381824 | bytes 17616896 | tf_op jit(solution)/shard_map/dot_general | solution.py:33
  73.0 25.4 %psum.14 = f32[896,8]{0,1:T(8,128)S(1)} all-reduce(f32[896,8]{0,1:T(8,128)S(1)} %fusion.25), channel_id=1, replica_groups=mesh['data'=8] {'data'}, use_global_device_ids=true, to_apply=%region_0.0 | all-reduce | flops 7168 | bytes 57344 | tf_op jit(solution)/shard_map/psum | solution.py:34
  98.4 14.3 %while.13 = (s32[]{:T(128)}, f32[896,8]{0,1:T(8,128)S(1)}, f32[896,8]{0,1:T(8,128)S(1)}, s32[]{:T(128)}, s32[]{:T(128)}) while((s32[]{:T(128)}, f32[896,8]{0,1:T(8,128)S(1)}, f32[896,8]{0,1:T(8,128)S(1)}, s32[]{:T(128)}, s32[]{:T(128)}) %tuple.36), condition=%wide.region_3.0_spmd, body=%wide.region_1.0_spmd.sunk | while | flops 175617 | bytes 82593 | solution.py:22
  98.4 0.2 convolution_bitcast_fusion.3
  98.6 0.8 multiply_reduce_fusion.2
  100.2 0.2 convolution_bitcast_fusion.3
  100.4 0.8 multiply_reduce_fusion.2
  102.0 0.2 convolution_bitcast_fusion.3
  102.2 0.8 multiply_reduce_fusion.2
  103.8 0.2 convolution_bitcast_fusion.3
  104.0 0.8 multiply_reduce_fusion.2
  105.6 0.2 convolution_bitcast_fusion.3
  105.7 0.8 multiply_reduce_fusion.2
  107.4 0.2 convolution_bitcast_fusion.3
  107.5 0.8 multiply_reduce_fusion.2
  109.3 0.8 multiply_reduce_fusion.2
  111.1 0.8 multiply_reduce_fusion.2
  112.7 20.2 %fusion.26 = f32[4864,8]{0,1:T(8,128)} fusion(f32[896,4864]{0,1:T(8,128)} %bitcast_add_fusion, f32[896,8]{0,1:T(8,128)S(1)} %get-tuple-element.68), kind=kOutput, calls=%fused_computation.37 | convolution fusion | flops 418381824 | bytes 17616896 | tf_op jit(solution)/shard_map/dot_general | solution.py:36
  132.9 43.4 %all-reduce.2.cloned.1.call-done = f32[4864,8]{0,1:T(8,128)} async-done(((f32[4864,8]{0,1:T(8,128)}), f32[4864,8]{0,1:T(8,128)}) %all-reduce.2.cloned.1.call-update) | async-done | bytes 155664 | tf_op jit(solution)/shard_map/psum | solution.py:37
  176.3 0.9 broadcast_multiply_fusion
  177.2 21.2 %subtract_bitcast_fusion = f32[1,896,4864]{1,2,0:T(8,128)} fusion(f32[896,4864]{0,1:T(8,128)} %bitcast_add_fusion, f32[896,8]{0,1:T(8,128)S(1)} %get-tuple-element.68, f32[4864,8]{0,1:T(8,128)S(1)} %broadcast_multiply_fusion), kind=kOutput, calls=%fused_computation.23 | convolution fusion | flops 422739968 | bytes 35049472 | tf_op jit(solution)/shard_map/dot_general | solution.py:38
  198.4 18.9 %copy.10 = f32[1,896,4864]{2,1,0:T(8,128)} copy(f32[1,896,4864]{1,2,0:T(8,128)} %subtract_bitcast_fusion) | data formatting | bytes 34865152
  (31 shorter events, 1.2 us)
Async XLA Ops:
  7.2 19.1 %copy-start = (bf16[1024,896]{1,0:T(8,128)(2,1)S(1)}, bf16[1024,896]{1,0:T(8,128)(2,1)}, u32[]{:S(2)}) copy-start(bf16[1024,896]{1,0:T(8,128)(2,1)} %param.7) | copy-start | bytes 5505028
  7.2 169.1 %all-reduce.2.cloned.1.call-start = ((), (), s32[]{:S(2)}) async-start(), calls=%async_computation | async-start | bytes 311296 | tf_op jit(solution)/shard_map/psum | solution.py:37
  26.2 33.3 %copy-start.4 = (f32[4864,8]{0,1:T(8,128)S(1)}, f32[4864,8]{0,1:T(8,128)}, u32[]{:S(2)}) copy-start(f32[4864,8]{0,1:T(8,128)} %param.10) | copy-start | bytes 466948
  112.7 85.7 %copy-start.2 = (f32[896,8]{0,1:T(8,128)}, f32[896,8]{0,1:T(8,128)S(1)}, u32[]{:S(2)}) copy-start(f32[896,8]{0,1:T(8,128)S(1)} %get-tuple-element.68) | copy-start | bytes 86020
  177.2 21.2 %copy-start.3 = (f32[4864,8]{0,1:T(8,128)}, f32[4864,8]{0,1:T(8,128)S(1)}, u32[]{:S(2)}) copy-start(f32[4864,8]{0,1:T(8,128)S(1)} %broadcast_multiply_fusion) | copy-start | bytes 466948
  177.2 40.0 %copy-start.1 = (bf16[1024,896]{1,0:T(8,128)(2,1)S(1)}, bf16[1024,896]{1,0:T(8,128)(2,1)}, u32[]{:S(2)}) copy-start(bf16[1024,896]{1,0:T(8,128)(2,1)} %param.7) | copy-start | bytes 5505028
Sparse Core Ops, SparseCore 0:
  133.1 43.1 all-reduce.1
where the time goes:
time: 225 us; the launch traced here: 224 us
  matrix products  95.8 us (43%)
  waiting for transfers between devices  43.4 us (19%)
  local copies, waits for them, and re-layouts  38.7 us (17%)
  blocking collectives  25.4 us (11%)
  between operations  14.1 us (6%)
  loops' own time  5.79 us (3%)
    psum x1, waiting for transfers between devices, per_device(): q_factor = lax.psum(q_part, 'data') / group_size  43.4 us
    unnamed x12, local copies, waits for them, and re-layouts  37.9 us
    dot_general x1, matrix products, per_device(): lax.dot_general(act_in, grad_pre, (((0,), (0,)), ((), ())), preferred_ele...  33.3 us
    psum x1, blocking collectives, per_device(): p_sum = lax.psum(p_part, 'data')  25.4 us
    dot_general x1, matrix products, per_device(): lax.dot_general(p_factor, q_factor, (((1,), (1,)), ((), ())), precision=E...  21.2 us
    dot_general x1, matrix products, per_device(): lax.dot_general(merged, p_factor, (((0,), (0,)), ((), ())), precision=EXA...  20.2 us
    dot_general x1, matrix products, per_device(): p_part = jnp.dot(merged, q_init, precision=EXACT_PREC)  13.5 us
    dot_general x8, matrix products, gs_step(): residual = column - jnp.dot(ortho_cols, proj_coef.T, precision=EXACT_PREC)  6.44 us
  transfers between devices with their start and end apart: 1, of which 1 were waited for; matrix products, arithmetic and copies ran while one was open for 0% of the time, Pallas kernels for 0%

commit v1 on v0

v1 whole, which is shorter than its diff:
```python
import functools
import jax
import jax.numpy as jnp
from jax import lax
from jax.experimental import pallas as pl
from jax.experimental.pallas import tpu as pltpu
from jax.sharding import PartitionSpec as P

F32 = jnp.float32
BF16 = jnp.bfloat16
GROUP = 8
ROWS = 1024
D_IN = 896
D_OUT = 4864
RANK = 8
CHUNK = 256
N_CHUNK = D_OUT // CHUNK
HALF = D_OUT // 2
PIECES = ((0, 512), (512, 512), (1024, 512), (1536, 512), (2048, 384))
AHEAD = 6
MESH = pl.DeviceIdType.MESH
C0 = 0.7978845608028654
C1 = 0.044715


def split3(x):
    hi = x.astype(BF16)
    rest = x - hi.astype(F32)
    mid = rest.astype(BF16)
    low = (rest - mid.astype(F32)).astype(BF16)
    return hi, mid, low


def stack3(x):
    hi, mid, low = split3(x)
    return jnp.concatenate([hi.astype(F32), mid.astype(F32), low.astype(F32)], axis=0).astype(BF16)


def gelu_grad_times(z, dy):
    x = z.astype(F32)
    sq = x * x
    t = jnp.tanh(x * (C0 + (C0 * C1) * sq))
    s = 0.5 + 0.5 * t
    w = x * (2.0 * C0 + (6.0 * C0 * C1) * sq)
    return (s * (1.0 + (1.0 - s) * w) * dy.astype(F32)).astype(BF16)


def orthonormal_rows(p0):
    p0 = p0 / jnp.max(jnp.abs(p0), axis=1, keepdims=True)
    row = lax.broadcasted_iota(jnp.int32, (RANK, 1), 0)
    cur = p0
    for k in range(RANK):
        v = jnp.broadcast_to(cur[k:k + 1, :], cur.shape)
        inv = lax.rsqrt(jnp.sum(v * v, axis=1, keepdims=True))
        coef = jnp.sum(v * p0, axis=1, keepdims=True) * inv
        q = v * inv
        cur = jnp.where(row == k, q, cur - jnp.where(row > k, coef, 0.0) * q)
    return cur


def main_kernel(a_ref, z_hbm, dy_hbm, qt_ref, e_hbm, m_ref, pt_ref, qn_ref,
                z_v, dy_v, at_ref, g0_ref, g1_ref, pacc_ref, p_all, q_part, q_pair, q_all,
                sem_in, sem_ps, sem_pr, sem_q1, sem_q2s, sem_q2r, sem_q3):
    me = lax.axis_index('data')
    core = lax.rem(me, 2)
    chip = me // 2
    mate = me + 1 - 2 * core

    barrier = pltpu.get_barrier_semaphore()
    for d in range(1, GROUP):
        pl.semaphore_signal(barrier, inc=1, device_id=(lax.rem(me + d, GROUP),), device_id_type=MESH)

    def fetch(c, go):
        cols = pl.ds(pl.multiple_of(c * CHUNK, CHUNK), CHUNK)
        for k, (src, dst) in enumerate(((z_hbm, z_v), (dy_hbm, dy_v), (e_hbm, m_ref))):
            go(pltpu.make_async_copy(src.at[:, cols], dst.at[:, cols], sem_in.at[k, c]), k)

    def start(c):
        fetch(c, lambda cp, k: cp.start())

    def wait_zy(c):
        fetch(c, lambda cp, k: cp.wait() if k < 2 else None)

    def wait_e(c):
        fetch(c, lambda cp, k: cp.wait() if k == 2 else None)

    for c in range(AHEAD):
        start(c)
    at_ref[...] = a_ref[...].T
    pacc_ref[...] = jnp.zeros_like(pacc_ref)

    def make_g(c, g_ref):
        cols = pl.ds(pl.multiple_of(c * CHUNK, CHUNK), CHUNK)
        for r in range(0, ROWS, 64):
            rows = pl.ds(r, 64)
            g_ref[rows, :] = gelu_grad_times(z_v[rows, cols], dy_v[rows, cols])

    def use_g(c, g_ref):
        cols = pl.ds(pl.multiple_of(c * CHUNK, CHUNK), CHUNK)
        q3 = stack3(qt_ref[:, cols])
        m = jnp.dot(at_ref[...], g_ref[...], preferred_element_type=F32) * (1.0 / ROWS) + m_ref[:, cols]
        m_ref[:, cols] = m
        dims = (((1,), (1,)), ((), ()))
        acc = None
        for piece in split3(m):
            part = lax.dot_general(q3, piece, dims, preferred_element_type=F32)
            acc = part if acc is None else acc + part
        pacc_ref[...] += acc

    wait_zy(0)
    make_g(0, g0_ref)

    def pair(i, carry):
        for k, (now, later) in enumerate(((g0_ref, g1_ref), (g1_ref, g0_ref))):
            c = 2 * i + k

            @pl.when(c + AHEAD < N_CHUNK)
            def _():
                start(c + AHEAD)

            wait_zy(c + 1)
            wait_e(c)
            make_g(c + 1, later)
            use_g(c, now)
        return carry

    lax.fori_loop(0, N_CHUNK // 2, pair, 0)
    wait_e(N_CHUNK - 1)
    use_g(N_CHUNK - 1, g0_ref)

    pacc = pacc_ref[...]
    p_all[me] = pacc[0:8] + pacc[8:16] + pacc[16:24]
    pl.semaphore_wait(barrier, GROUP - 1)

    def p_copy(d):
        return pltpu.make_async_remote_copy(
            src_ref=p_all.at[me], dst_ref=p_all.at[me], send_sem=sem_ps.at[d], recv_sem=sem_pr.at[d],
            device_id=(lax.rem(me + d, GROUP),), device_id_type=MESH)

    for d in range(1, GROUP):
        p_copy(d).start()
    for d in range(1, GROUP):
        p_copy(d).wait()
    p_sum = p_all[0]
    for d in range(1, GROUP):
        p_sum = p_sum + p_all[d]
    p_t = orthonormal_rows(p_sum)
    pt_ref[...] = p_t
    p3 = stack3(p_t)

    def q_block(half, off, width):
        cols = pl.ds(pl.multiple_of(half * HALF + off, 128), width)
        acc = None
        for piece in split3(m_ref[:, cols]):
            part = jnp.dot(p3, piece, preferred_element_type=F32)
            acc = part if acc is None else acc + part
        return acc[0:8] + acc[8:16] + acc[16:24]

    for off, width in PIECES:
        q_part[:, off:off + width] = q_block(1 - core, off, width)
    to_mate = pltpu.make_async_remote_copy(
        src_ref=q_part, dst_ref=q_pair, send_sem=sem_q1.at[0], recv_sem=sem_q1.at[1],
        device_id=(mate,), device_id_type=MESH)
    to_mate.start()
    own = [q_block(core, off, width) for off, width in PIECES]
    to_mate.wait()
    for (off, width), val in zip(PIECES, own):
        q_all[chip, :, off:off + width] = val + q_pair[:, off:off + width]

    def q_copy(d):
        return pltpu.make_async_remote_copy(
            src_ref=q_all.at[chip], dst_ref=q_all.at[chip], send_sem=sem_q2s.at[d], recv_sem=sem_q2r.at[d],
            device_id=(lax.rem(me + 2 * d, GROUP),), device_id_type=MESH)

    for d in range(1, 4):
        q_copy(d).start()
    for d in range(1, 4):
        q_copy(d).wait()
    my_half = pl.ds(pl.multiple_of(core * HALF, 128), HALF)
    qn_ref[:, my_half] = (q_all[0] + q_all[1] + q_all[2] + q_all[3]) * (1.0 / GROUP)
    done = pltpu.make_async_remote_copy(
        src_ref=qn_ref.at[:, my_half], dst_ref=qn_ref.at[:, my_half], send_sem=sem_q3.at[0],
        recv_sem=sem_q3.at[1], device_id=(mate,), device_id_type=MESH)
    done.start()
    done.wait()


def error_kernel(pt_ref, qn_ref, m_ref, e_ref, po_ref, qo_ref):
    @pl.when(pl.program_id(0) == 0)
    def _():
        po_ref[...] = pt_ref[...]

    qo_ref[...] = qn_ref[...]

    def order(parts):
        return jnp.concatenate([p.astype(F32) for p in parts], axis=0).astype(BF16)

    ph, pm, pl_ = split3(pt_ref[...])
    qh, qm, ql = split3(qn_ref[...])
    left = order((ph, ph, ph, pm, pm, pl_))
    right = order((qh, qm, ql, qh, qm, qh))
    est = lax.dot_general(left, right, (((0,), (0,)), ((), ())), preferred_element_type=F32)
    cols = pl.ds(pl.multiple_of(pl.program_id(0) * e_ref.shape[1], 128), e_ref.shape[1])
    e_ref[...] = m_ref[:, cols] - est


def per_device(act_in, pre_act, grad_out, q_init, err_mem):
    vm = pl.BlockSpec(memory_space=pltpu.VMEM)
    anyspec = pl.BlockSpec(memory_space=pl.ANY)
    merged, p_t, qn_t = pl.pallas_call(
        main_kernel,
        out_shape=(pltpu.VMEM((D_IN, D_OUT), F32), pltpu.VMEM((RANK, D_IN), F32), pltpu.VMEM((RANK, D_OUT), F32)),
        in_specs=[vm, anyspec, anyspec, vm, anyspec],
        out_specs=(vm, vm, vm),
        scratch_shapes=[
            pltpu.VMEM((ROWS, D_OUT), BF16),
            pltpu.VMEM((ROWS, D_OUT), BF16),
            pltpu.VMEM((D_IN, ROWS), BF16),
            pltpu.VMEM((ROWS, CHUNK), BF16),
            pltpu.VMEM((ROWS, CHUNK), BF16),
            pltpu.VMEM((3 * RANK, D_IN), F32),
            pltpu.VMEM((GROUP, RANK, D_IN), F32),
            pltpu.VMEM((RANK, HALF), F32),
            pltpu.VMEM((RANK, HALF), F32),
            pltpu.VMEM((4, RANK, HALF), F32),
            pltpu.SemaphoreType.DMA((3, N_CHUNK)),
            pltpu.SemaphoreType.DMA((GROUP,)),
            pltpu.SemaphoreType.DMA((GROUP,)),
            pltpu.SemaphoreType.DMA((2,)),
            pltpu.SemaphoreType.DMA((4,)),
            pltpu.SemaphoreType.DMA((4,)),
            pltpu.SemaphoreType.DMA((2,)),
        ],
        compiler_params=pltpu.CompilerParams(
            collective_id=0, has_side_effects=True, vmem_limit_bytes=VMEM1),
        name='merge_and_factor',
    )(act_in, pre_act, grad_out, q_init.T, err_mem.reshape(D_IN, D_OUT))
    bw = 256
    err_new, p_o, qn_o = pl.pallas_call(
        error_kernel,
        grid=(D_OUT // bw,),
        out_shape=(jax.ShapeDtypeStruct((D_IN, D_OUT), F32), jax.ShapeDtypeStruct((RANK, D_IN), F32),
                   jax.ShapeDtypeStruct((RANK, D_OUT), F32)),
        in_specs=[pl.BlockSpec((RANK, D_IN), lambda i: (0, 0)), pl.BlockSpec((RANK, bw), lambda i: (0, i)),
                  vm],
        out_specs=(pl.BlockSpec((D_IN, bw), lambda i: (0, i)), pl.BlockSpec((RANK, D_IN), lambda i: (0, 0)),
                   pl.BlockSpec((RANK, bw), lambda i: (0, i))),
        compiler_params=pltpu.CompilerParams(vmem_limit_bytes=VMEM2),
        name='new_error',
    )(p_t, qn_t, merged)
    return p_o.T, qn_o.T, err_new[None]


VMEM1 = 44 * 1024 * 1024
VMEM2 = 24 * 1024 * 1024


def solution(mesh):
    return jax.shard_map(
        per_device, mesh=mesh,
        in_specs=(P('data', None), P('data', None), P('data', None), P(None, None), P('data', None, None)),
        out_specs=(P(None, None), P(None, None), P('data', None, None)), check_vma=False)
```

time: 225 us -> 78.3 us (0.35)
  matrix products: 95.8 us -> 0 us
  Pallas kernels: 0 us -> 77.6 us
  waiting for transfers between devices: 43.4 us -> 0 us
  local copies, waits for them, and re-layouts: 38.7 us -> 0 us
  blocking collectives: 25.4 us -> 0 us
  between operations: 14.1 us -> 0.64 us
  loops' own time: 5.79 us -> 0 us
    dot_general x20 -> x0, matrix products: 95.8 us -> none  [the longest x1 33.3 us: per_device(): lax.dot_general(act_in, grad_pre, (((0,), (0,)), ((), ())), preferred_ele...]
    pallas_call x0 -> x2, Pallas kernels: none -> 77.6 us  [the longest x1 65.1 us: per_device(): pl.pallas_call(main_kernel, out_shape=(pltpu.VMEM((D_IN, D_OUT), F32), pl...]
    psum x1 -> x0, waiting for transfers between devices: 43.4 us -> none  [per_device(): q_factor = lax.psum(q_part, 'data') / group_size]
    unnamed x12 -> x0, local copies, waits for them, and re-layouts: 37.9 us -> none
    psum x1 -> x0, blocking collectives: 25.4 us -> none  [per_device(): p_sum = lax.psum(p_part, 'data')]
    another operation x1 -> x0, loops' own time: 5.79 us -> none  [orthonormalize(): return lax.fori_loop(0, p_sum.shape[1], gs_step, jnp.zeros_like(p_sum))]
  transfers between devices with their start and end apart: 1 -> 0, of which waited for: 1 -> 0; matrix products, arithmetic and copies ran while one was open for 0% -> 0% of each run, Pallas kernels for 0% -> 0%
where the time goes in v1:
time: 78.3 us; the launch traced here: 78.2 us
  Pallas kernels  77.6 us (99%)
    pallas_call x1, Pallas kernels, per_device(): pl.pallas_call(main_kernel, out_shape=(pltpu.VMEM((D_IN, D_OUT), F32), pl...  65.1 us
    pallas_call x1, Pallas kernels, per_device(): pl.pallas_call(error_kernel, grid=(D_OUT // bw,), out_shape=(jax.ShapeDty...  12.4 us

profile of v1, /device:TPU:0, one launch (start us, length us, event | category | flops | bytes accessed | tf_op | source)
XLA Modules:
  0.0 78.2 jit_solution(3814574207713684584)
XLA Ops:
  0.6 65.1 %merge_and_factor.1 = (f32[896,4864]{1,0:T(8,128)S(1)}, f32[8,896]{1,0:T(8,128)S(1)}, f32[8,4864]{1,0:T(8,128)S(1)}) custom-call(bf16[1024,896]{1,0:T(8,128)(2,1)} %a_ref.1, bf16[1024,4864]{1,0:T(8,128)(2,1)} %z_hbm.1, bf16[1024,4864]{1,0:T(8,128)(2,1)} %dy_hbm.1, f32[8,4864]{1,0:T(8,128)} %bitcast.6, f32[896,4864]{1,0:T(8,128)} %bitcast.5), custom_call_target="tpu_custom_call" | custom-call | tf_op jit(solution)/shard_map/merge_and_factor/pallas_call | solution.py:210
  65.8 12.4 %new_error.1 = (f32[896,4864]{1,0:T(8,128)}, f32[8,896]{1,0:T(8,128)}, f32[8,4864]{1,0:T(8,128)}) custom-call(f32[8,896]{1,0:T(8,128)S(1)} %get-tuple-element.9.pt_ref, f32[8,4864]{1,0:T(8,128)S(1)} %get-tuple-element.10.qn_ref, f32[896,4864]{1,0:T(8,128)S(1)} %get-tuple-element.11.m_ref), custom_call_target="tpu_custom_call" | custom-call | tf_op jit(solution)/shard_map/new_error/pallas_call | solution.py:239

commit v2 on v1

v2 whole, which is shorter than its diff:
```python
import jax
import jax.numpy as jnp
from jax import lax
from jax.experimental import pallas as pl
from jax.experimental.pallas import tpu as pltpu
from jax.sharding import PartitionSpec as P

F32 = jnp.float32
BF16 = jnp.bfloat16
GROUP = 8
ROWS = 1024
D_IN = 896
D_OUT = 4864
RANK = 8
LANES = 128
CHUNK = 256
N_CHUNK = D_OUT // CHUNK
HALF = D_OUT // 2
SIDE = D_IN // 2
SLAB = 64
SLABS = SIDE // SLAB
PADDED = 4 * RANK
AHEAD = 6
MESH = pl.DeviceIdType.MESH
C0 = 0.7978845608028654
C1 = 0.044715
VMEM_MERGE = 44 * 1024 * 1024
VMEM_FACTOR = 20 * 1024 * 1024
VMEM_ERROR = 20 * 1024 * 1024


def split3(x):
    hi = x.astype(BF16)
    rest = x - hi.astype(F32)
    mid = rest.astype(BF16)
    low = (rest - mid.astype(F32)).astype(BF16)
    return hi, mid, low


def stacked(parts):
    return jnp.concatenate([p.astype(F32) for p in parts], axis=0).astype(BF16)


def gelu_grad_times(z, dy):
    x = z.astype(F32)
    sq = x * x
    s = lax.logistic(x * (2.0 * C0 + (2.0 * C0 * C1) * sq))
    r = 2.0 * C0 + (6.0 * C0 * C1) * sq
    return (s * (1.0 + ((1.0 - s) * x) * r) * dy.astype(F32)).astype(BF16)


def orthonormal_rows(p0):
    p0 = p0 / jnp.max(jnp.abs(p0), axis=1, keepdims=True)
    row = lax.broadcasted_iota(jnp.int32, (RANK, 1), 0)
    cur = p0
    for k in range(RANK):
        v = jnp.broadcast_to(cur[k:k + 1, :], cur.shape)
        inv = lax.rsqrt(jnp.sum(v * v, axis=1, keepdims=True))
        coef = jnp.sum(v * p0, axis=1, keepdims=True) * inv
        q = v * inv
        cur = jnp.where(row == k, q, cur - jnp.where(row > k, coef, 0.0) * q)
    return cur


def wide(ref, first, rows):
    return jnp.concatenate([ref[first, rows, :], ref[first + 1, rows, :]], axis=1)


def merge_kernel(a_hbm, z_hbm, dy_hbm, qt_ref, e_hbm, m_ref, p_ref,
                 a_v, z_v, dy_v, at_ref, g0, g1, pc0, pc1, sem_in, sem_a):
    gs = (g0, g1)
    pieces = (pc0, pc1)

    def cols_of(c):
        return pl.ds(c * CHUNK if isinstance(c, int) else pl.multiple_of(c * CHUNK, CHUNK), CHUNK)

    def copy(k, c):
        src, dst = ((z_hbm, z_v), (dy_hbm, dy_v), (e_hbm, m_ref))[k]
        return pltpu.make_async_copy(src.at[:, cols_of(c)], dst.at[:, cols_of(c)], sem_in.at[k, c])

    def start(c):
        for k in range(3):
            copy(k, c).start()

    def gelu_slab(c, j):
        rows = pl.ds(j * SLAB, SLAB)
        g = gelu_grad_times(z_v[rows, cols_of(c)], dy_v[rows, cols_of(c)])
        for b in range(2):
            gs[c_par(c)][b, rows, :] = g[:, b * LANES:(b + 1) * LANES]

    par_box = [0]

    def c_par(c):
        return par_box[0] ^ 1

    def body_of(accs, p_acc):
        def merge_slab(c, par, q, i):
            rows = pl.ds(q * SIDE + i * SLAB, SLAB)
            m = pltpu.matmul_pop(accs[par][q][i]) * (1.0 / ROWS) + m_ref[rows, cols_of(c)]
            m_ref[rows, cols_of(c)] = m
            for t, piece in enumerate(split3(m)):
                for b in range(2):
                    pieces[par][t, b, rows, :] = piece[:, b * LANES:(b + 1) * LANES]

        def grad_step(par, q, k):
            pltpu.matmul_push_rhs(wide(gs[par], 0, pl.ds(k * CHUNK, CHUNK)), staging_register=0, mxu_index=q)
            for i in range(SLABS):
                lhs = wide(at_ref, 2 * k, pl.ds(q * SIDE + i * SLAB, SLAB))
                pltpu.matmul_acc_lhs(accs[par][q][i], lhs, load_staged_rhs=0 if i == 0 else None)

        def rank_step(q3, par, q, blk, t):
            rows = pl.ds(q * SIDE + blk * (SIDE - CHUNK), CHUNK)
            tile = jnp.concatenate([pieces[par][t, 0, rows, :], pieces[par][t, 1, rows, :]], axis=1)
            pltpu.matmul_push_rhs(tile, staging_register=1, mxu_index=q, transpose=True)
            pltpu.matmul_acc_lhs(p_acc[q][blk], q3, load_staged_rhs=1)

        def step(c, par, gelu, grad, merge, rank):
            par_box[0] = par
            if gelu:
                copy(0, c + 1).wait()
                copy(1, c + 1).wait()
            if merge:
                copy(2, c - 1).wait()
            if rank:
                qt = qt_ref[:, cols_of(c - 2)]
                q3 = stacked(split3(qt) + (jnp.zeros_like(qt),))
            tiles = [(blk, t) for blk in range(2) for t in range(3)]
            mxu = []
            for k in range(4):
                if grad:
                    mxu.append(lambda q, k=k: grad_step(par, q, k))
                for n, (blk, t) in enumerate(tiles):
                    if rank and n * 4 // len(tiles) == k:
                        mxu.append(lambda q, blk=blk, t=t: rank_step(q3, par, q, blk, t))
            n_gelu = ROWS // SLAB
            for s in range(SLABS):
                for n, op in enumerate(mxu):
                    if n * SLABS // len(mxu) == s:
                        op(0)
                        op(1)
                if merge:
                    merge_slab(c - 1, par ^ 1, 0, s)
                    merge_slab(c - 1, par ^ 1, 1, s)
                if gelu:
                    for j in range(n_gelu):
                        if j * SLABS // n_gelu == s:
                            gelu_slab(c + 1, j)

        load_a = pltpu.make_async_copy(a_hbm, a_v, sem_a)
        load_a.start()
        for c in range(AHEAD):
            start(c)
        load_a.wait()
        for b in range(ROWS // LANES):
            at_ref[b] = a_v[b * LANES:(b + 1) * LANES, :].T
        step(-1, 1, True, False, False, False)
        start(AHEAD)
        step(0, 0, True, True, False, False)
        start(AHEAD + 1)
        step(1, 1, True, True, True, False)

        def pair(i, carry):
            for par in range(2):
                c = 2 * i + par

                @pl.when(c + AHEAD < N_CHUNK)
                def _():
                    start(c + AHEAD)

                step(c, par, True, True, True, True)
            return carry

        lax.fori_loop(1, N_CHUNK // 2, pair, 0)
        step(N_CHUNK - 1, 0, False, True, True, True)
        step(N_CHUNK, 1, False, False, True, True)
        step(N_CHUNK + 1, 0, False, False, False, True)
        skip = 2 * CHUNK - SIDE
        out = []
        for q in range(2):
            for blk in range(2):
                p3 = pltpu.matmul_pop(p_acc[q][blk])
                part = p3[0:8] + p3[8:16] + p3[16:24]
                out.append(part[:, skip:] if blk else part)
        p_ref[...] = jnp.concatenate(out, axis=1)

    def acc(q, rows):
        return pltpu.ACC(q)((rows, CHUNK), F32)

    pl.run_scoped(
        body_of,
        tuple(tuple(tuple(acc(q, SLAB) for _ in range(SLABS)) for q in range(2)) for _ in range(2)),
        tuple(tuple(acc(q, PADDED) for _ in range(2)) for q in range(2)))


def factor_kernel(p_ref, m_ref, pt_ref, qn_ref, p_all, pc0, pc1, q_part, q_pair, q_all,
                  sem_ps, sem_pr, sem_q1, sem_q2s, sem_q2r, sem_q3):
    me = lax.axis_index('data')
    core = lax.rem(me, 2)
    chip = me // 2
    mate = me + 1 - 2 * core
    pieces = (pc0, pc1)

    barrier = pltpu.get_barrier_semaphore()
    for d in range(1, GROUP):
        pl.semaphore_signal(barrier, inc=1, device_id=(lax.rem(me + d, GROUP),), device_id_type=MESH)
    p_all[me] = p_ref[...]
    pl.semaphore_wait(barrier, GROUP - 1)

    def p_copy(d):
        return pltpu.make_async_remote_copy(
            src_ref=p_ref, dst_ref=p_all.at[me], send_sem=sem_ps.at[d], recv_sem=sem_pr.at[d],
            device_id=(lax.rem(me + d, GROUP),), device_id_type=MESH)

    for d in range(1, GROUP):
        p_copy(d).start()
    for d in range(1, GROUP):
        p_copy(d).wait()
    p_sum = p_all[0]
    for d in range(1, GROUP):
        p_sum = p_sum + p_all[d]
    p_t = orthonormal_rows(p_sum)
    pt_ref[...] = p_t
    p3 = stacked(split3(p_t))

    def split_block(half, off, width, par):
        cols = pl.ds(pl.multiple_of(half * HALF + off, LANES), width)
        for r in range(0, D_IN, SLAB):
            rows = pl.ds(r, SLAB)
            for t, piece in enumerate(split3(m_ref[rows, cols])):
                for b in range(width // LANES):
                    pieces[par][t, b, rows, :] = piece[:, b * LANES:(b + 1) * LANES]

    def q_block(width, par):
        acc = None
        for t in range(3):
            tile = jnp.concatenate([pieces[par][t, b] for b in range(width // LANES)], axis=1)
            part = jnp.dot(p3, tile, preferred_element_type=F32)
            acc = part if acc is None else acc + part
        return acc[0:8] + acc[8:16] + acc[16:24]

    blocks = [(off, min(CHUNK, HALF - off)) for off in range(0, HALF, CHUNK)]
    work = [(1 - core, off, width) for off, width in blocks] + [(core, off, width) for off, width in blocks]
    to_mate = pltpu.make_async_remote_copy(
        src_ref=q_part, dst_ref=q_pair, send_sem=sem_q1.at[0], recv_sem=sem_q1.at[1],
        device_id=(mate,), device_id_type=MESH)
    own = []
    split_block(*work[0], 0)
    for n, (half, off, width) in enumerate(work):
        if n + 1 < len(work):
            split_block(*work[n + 1], (n + 1) % 2)
        val = q_block(width, n % 2)
        if n < len(blocks):
            q_part[:, off:off + width] = val
            if n == len(blocks) - 1:
                to_mate.start()
        else:
            own.append(val)
    to_mate.wait()
    for (off, width), val in zip(blocks, own):
        q_all[chip, :, off:off + width] = val + q_pair[:, off:off + width]

    def q_copy(d):
        return pltpu.make_async_remote_copy(
            src_ref=q_all.at[chip], dst_ref=q_all.at[chip], send_sem=sem_q2s.at[d], recv_sem=sem_q2r.at[d],
            device_id=(lax.rem(me + 2 * d, GROUP),), device_id_type=MESH)

    for d in range(1, 4):
        q_copy(d).start()
    for d in range(1, 4):
        q_copy(d).wait()
    my_half = pl.ds(pl.multiple_of(core * HALF, LANES), HALF)
    qn_ref[:, my_half] = (q_all[0] + q_all[1] + q_all[2] + q_all[3]) * (1.0 / GROUP)
    done = pltpu.make_async_remote_copy(
        src_ref=qn_ref.at[:, my_half], dst_ref=qn_ref.at[:, my_half], send_sem=sem_q3.at[0],
        recv_sem=sem_q3.at[1], device_id=(mate,), device_id_type=MESH)
    done.start()
    done.wait()


def error_kernel(pt_ref, qn_ref, m_ref, e_ref, po_ref, qo_ref, left_ref, right_ref):
    @pl.when(pl.program_id(0) == 0)
    def _():
        po_ref[...] = pt_ref[...]
        qo_ref[...] = qn_ref[...]
        ph, pm, pl_ = split3(pt_ref[...])
        qh, qm, ql = split3(qn_ref[...])
        left_ref[...] = stacked((ph, ph, ph, pm, pm, pl_)).T
        right_ref[...] = stacked((qh, qm, ql, qh, qm, qh))

    n = e_ref.shape[0]
    rows = pl.ds(pl.multiple_of(pl.program_id(0) * n, 16), n)
    est = jnp.dot(left_ref[rows, :], right_ref[...], preferred_element_type=F32)
    e_ref[...] = m_ref[rows, :] - est


def per_device(act_in, pre_act, grad_out, q_init, err_mem):
    vm = pl.BlockSpec(memory_space=pltpu.VMEM)
    anyspec = pl.BlockSpec(memory_space=pl.ANY)
    merged, p_part = pl.pallas_call(
        merge_kernel,
        out_shape=(pltpu.VMEM((D_IN, D_OUT), F32), pltpu.VMEM((RANK, D_IN), F32)),
        in_specs=[anyspec, anyspec, anyspec, vm, anyspec],
        out_specs=(vm, vm),
        scratch_shapes=[
            pltpu.VMEM((ROWS, D_IN), BF16),
            pltpu.VMEM((ROWS, D_OUT), BF16),
            pltpu.VMEM((ROWS, D_OUT), BF16),
            pltpu.VMEM((ROWS // LANES, D_IN, LANES), BF16),
            pltpu.VMEM((2, ROWS, LANES), BF16),
            pltpu.VMEM((2, ROWS, LANES), BF16),
            pltpu.VMEM((3, 2, D_IN, LANES), BF16),
            pltpu.VMEM((3, 2, D_IN, LANES), BF16),
            pltpu.SemaphoreType.DMA((3, N_CHUNK)),
            pltpu.SemaphoreType.DMA,
        ],
        compiler_params=pltpu.CompilerParams(vmem_limit_bytes=VMEM_MERGE),
        name='merge',
    )(act_in, pre_act, grad_out, q_init.T, err_mem.reshape(D_IN, D_OUT))
    p_t, qn_t = pl.pallas_call(
        factor_kernel,
        out_shape=(pltpu.VMEM((RANK, D_IN), F32), pltpu.VMEM((RANK, D_OUT), F32)),
        in_specs=[vm, vm],
        out_specs=(vm, vm),
        scratch_shapes=[
            pltpu.VMEM((GROUP, RANK, D_IN), F32),
            pltpu.VMEM((3, 2, D_IN, LANES), BF16),
            pltpu.VMEM((3, 2, D_IN, LANES), BF16),
            pltpu.VMEM((RANK, HALF), F32),
            pltpu.VMEM((RANK, HALF), F32),
            pltpu.VMEM((4, RANK, HALF), F32),
            pltpu.SemaphoreType.DMA((GROUP,)),
            pltpu.SemaphoreType.DMA((GROUP,)),
            pltpu.SemaphoreType.DMA((2,)),
            pltpu.SemaphoreType.DMA((4,)),
            pltpu.SemaphoreType.DMA((4,)),
            pltpu.SemaphoreType.DMA((2,)),
        ],
        compiler_params=pltpu.CompilerParams(
            collective_id=0, has_side_effects=True, vmem_limit_bytes=VMEM_FACTOR),
        name='factor',
    )(p_part, merged)
    bh = 112
    err_new, p_o, qn_o = pl.pallas_call(
        error_kernel,
        grid=(D_IN // bh,),
        out_shape=(jax.ShapeDtypeStruct((D_IN, D_OUT), F32), jax.ShapeDtypeStruct((RANK, D_IN), F32),
                   jax.ShapeDtypeStruct((RANK, D_OUT), F32)),
        in_specs=[vm, vm, vm],
        out_specs=(pl.BlockSpec((bh, D_OUT), lambda i: (i, 0)), pl.BlockSpec((RANK, D_IN), lambda i: (0, 0)),
                   pl.BlockSpec((RANK, D_OUT), lambda i: (0, 0))),
        scratch_shapes=[pltpu.VMEM((D_IN, 6 * RANK), BF16), pltpu.VMEM((6 * RANK, D_OUT), BF16)],
        compiler_params=pltpu.CompilerParams(vmem_limit_bytes=VMEM_ERROR),
        name='new_error',
    )(p_t, qn_t, merged)
    return p_o.T, qn_o.T, err_new[None]


def solution(mesh):
    return jax.shard_map(
        per_device, mesh=mesh,
        in_specs=(P('data', None), P('data', None), P('data', None), P(None, None), P('data', None, None)),
        out_specs=(P(None, None), P(None, None), P('data', None, None)), check_vma=False)
```

time: 78.3 us -> 66 us (0.84)
  Pallas kernels: 77.6 us -> 65.2 us
    pallas_call x2 -> x3, Pallas kernels: 77.6 us -> 65.2 us  [the longest x1 34.6 us: per_device(): pl.pallas_call(merge_kernel, out_shape=(pltpu.VMEM((D_IN, D_OUT), F32), p...]
where the time goes in v2:
time: 66 us; the launch traced here: 65.9 us
  Pallas kernels  65.2 us (99%)
    pallas_call x1, Pallas kernels, per_device(): pl.pallas_call(merge_kernel, out_shape=(pltpu.VMEM((D_IN, D_OUT), F32), p...  34.6 us
    pallas_call x1, Pallas kernels, per_device(): pl.pallas_call(factor_kernel, out_shape=(pltpu.VMEM((RANK, D_IN), F32), p...  22.7 us
    pallas_call x1, Pallas kernels, per_device(): pl.pallas_call(error_kernel, grid=(D_IN // bh,), out_shape=(jax.ShapeDtyp...  7.97 us

profile of v2, /device:TPU:0, one launch (start us, length us, event | category | flops | bytes accessed | tf_op | source)
XLA Modules:
  0.0 65.9 jit_solution(12087213879018846559)
XLA Ops:
  0.6 34.6 %merge.1 = (f32[896,4864]{1,0:T(8,128)S(1)}, f32[8,896]{1,0:T(8,128)S(1)}) custom-call(bf16[1024,896]{1,0:T(8,128)(2,1)} %a_hbm.1, bf16[1024,4864]{1,0:T(8,128)(2,1)} %z_hbm.1, bf16[1024,4864]{1,0:T(8,128)(2,1)} %dy_hbm.1, f32[8,4864]{1,0:T(8,128)} %bitcast.6, f32[896,4864]{1,0:T(8,128)} %bitcast.5), custom_call_target="tpu_custom_call" | custom-call | tf_op jit(solution)/shard_map/merge/pallas_call | solution.py:299
  35.2 22.7 %factor.1 = (f32[8,896]{1,0:T(8,128)S(1)}, f32[8,4864]{1,0:T(8,128)S(1)}) custom-call(f32[8,896]{1,0:T(8,128)S(1)} %get-tuple-element.10.p_ref, f32[896,4864]{1,0:T(8,128)S(1)} %get-tuple-element.11.m_ref), custom_call_target="tpu_custom_call" | custom-call | tf_op jit(solution)/shard_map/factor/pallas_call | solution.py:319
  57.9 8.0 %new_error.1 = (f32[896,4864]{1,0:T(8,128)}, f32[8,896]{1,0:T(8,128)}, f32[8,4864]{1,0:T(8,128)}) custom-call(f32[8,896]{1,0:T(8,128)S(1)} %get-tuple-element.12.pt_ref, f32[8,4864]{1,0:T(8,128)S(1)} %get-tuple-element.13.qn_ref, f32[896,4864]{1,0:T(8,128)S(1)} %get-tuple-element.11.m_ref), custom_call_target="tpu_custom_call" | custom-call | tf_op jit(solution)/shard_map/new_error/pallas_call | solution.py:343

commit v3 on v2

--- a/solution.py
+++ b/solution.py
@@ -67,7 +67,7 @@
 
 
 def merge_kernel(a_hbm, z_hbm, dy_hbm, qt_ref, e_hbm, m_ref, p_ref,
-                 a_v, z_v, dy_v, at_ref, g0, g1, pc0, pc1, sem_in, sem_a):
+                 a_v, z_v, dy_v, at_ref, q3_v, g0, g1, pc0, pc1, sem_in, sem_a):
     gs = (g0, g1)
     pieces = (pc0, pc1)
 
@@ -122,8 +122,7 @@
             if merge:
                 copy(2, c - 1).wait()
             if rank:
-                qt = qt_ref[:, cols_of(c - 2)]
-                q3 = stacked(split3(qt) + (jnp.zeros_like(qt),))
+                q3 = jnp.concatenate([q3_v[2 * (c - 2)], q3_v[2 * (c - 2) + 1]], axis=1)
             tiles = [(blk, t) for blk in range(2) for t in range(3)]
             mxu = []
             for k in range(4):
@@ -133,14 +132,15 @@
                     if rank and n * 4 // len(tiles) == k:
                         mxu.append(lambda q, blk=blk, t=t: rank_step(q3, par, q, blk, t))
             n_gelu = ROWS // SLAB
+            if merge:
+                for s in range(SLABS):
+                    merge_slab(c - 1, par ^ 1, 0, s)
+                    merge_slab(c - 1, par ^ 1, 1, s)
             for s in range(SLABS):
                 for n, op in enumerate(mxu):
                     if n * SLABS // len(mxu) == s:
                         op(0)
                         op(1)
-                if merge:
-                    merge_slab(c - 1, par ^ 1, 0, s)
-                    merge_slab(c - 1, par ^ 1, 1, s)
                 if gelu:
                     for j in range(n_gelu):
                         if j * SLABS // n_gelu == s:
@@ -150,10 +150,18 @@
         load_a.start()
         for c in range(AHEAD):
             start(c)
+        qt = qt_ref[...]
+        q_all = stacked(split3(qt) + (jnp.zeros_like(qt),))
+        for b in range(2 * N_CHUNK):
+            q3_v[b] = q_all[:, b * LANES:(b + 1) * LANES]
         load_a.wait()
+        copy(0, 0).wait()
+        copy(1, 0).wait()
+        par_box[0] = 1
         for b in range(ROWS // LANES):
             at_ref[b] = a_v[b * LANES:(b + 1) * LANES, :].T
-        step(-1, 1, True, False, False, False)
+            gelu_slab(0, 2 * b)
+            gelu_slab(0, 2 * b + 1)
         start(AHEAD)
         step(0, 0, True, True, False, False)
         start(AHEAD + 1)
@@ -167,7 +175,9 @@
                 def _():
                     start(c + AHEAD)
 
-                step(c, par, True, True, True, True)
+                @pl.when(c + 1 < N_CHUNK)
+                def _():
+                    step(c, par, True, True, True, True)
             return carry
 
         lax.fori_loop(1, N_CHUNK // 2, pair, 0)
@@ -306,6 +316,7 @@
             pltpu.VMEM((ROWS, D_OUT), BF16),
             pltpu.VMEM((ROWS, D_OUT), BF16),
             pltpu.VMEM((ROWS // LANES, D_IN, LANES), BF16),
+            pltpu.VMEM((2 * N_CHUNK, PADDED, LANES), BF16),
             pltpu.VMEM((2, ROWS, LANES), BF16),
             pltpu.VMEM((2, ROWS, LANES), BF16),
             pltpu.VMEM((3, 2, D_IN, LANES), BF16),
@@ -339,7 +350,7 @@
             collective_id=0, has_side_effects=True, vmem_limit_bytes=VMEM_FACTOR),
         name='factor',
     )(p_part, merged)
-    bh = 112
+    bh = 64
     err_new, p_o, qn_o = pl.pallas_call(
         error_kernel,
         grid=(D_IN // bh,),

time: 66 us -> 63.7 us (0.965)
  Pallas kernels: 65.2 us -> 62.9 us
    pallas_call x1, Pallas kernels: 34.6 us -> 30.3 us  [per_device(): pl.pallas_call(merge_kernel, out_shape=(pltpu.VMEM((D_IN, D_OUT), F32), p...]
    pallas_call x1, Pallas kernels: 7.97 us -> 9.93 us  [per_device(): pl.pallas_call(error_kernel, grid=(D_IN // bh,), out_shape=(jax.ShapeDtyp...]
where the time goes in v3:
time: 63.7 us; the launch traced here: 63.6 us
  Pallas kernels  62.9 us (99%)
  between operations  0.65 us (1%)
    pallas_call x1, Pallas kernels, per_device(): pl.pallas_call(merge_kernel, out_shape=(pltpu.VMEM((D_IN, D_OUT), F32), p...  30.3 us
    pallas_call x1, Pallas kernels, per_device(): pl.pallas_call(factor_kernel, out_shape=(pltpu.VMEM((RANK, D_IN), F32), p...  22.7 us
    pallas_call x1, Pallas kernels, per_device(): pl.pallas_call(error_kernel, grid=(D_IN // bh,), out_shape=(jax.ShapeDtyp...  9.93 us

profile of v3, /device:TPU:0, one launch (start us, length us, event | category | flops | bytes accessed | tf_op | source)
XLA Modules:
  0.0 63.6 jit_solution(7581496571529476584)
XLA Ops:
  0.6 30.3 %merge.1 = (f32[896,4864]{1,0:T(8,128)S(1)}, f32[8,896]{1,0:T(8,128)S(1)}) custom-call(bf16[1024,896]{1,0:T(8,128)(2,1)} %a_hbm.1, bf16[1024,4864]{1,0:T(8,128)(2,1)} %z_hbm.1, bf16[1024,4864]{1,0:T(8,128)(2,1)} %dy_hbm.1, f32[8,4864]{1,0:T(8,128)} %bitcast.6, f32[896,4864]{1,0:T(8,128)} %bitcast.5), custom_call_target="tpu_custom_call" | custom-call | tf_op jit(solution)/shard_map/merge/pallas_call | solution.py:309
  31.0 22.7 %factor.1 = (f32[8,896]{1,0:T(8,128)S(1)}, f32[8,4864]{1,0:T(8,128)S(1)}) custom-call(f32[8,896]{1,0:T(8,128)S(1)} %get-tuple-element.10.p_ref, f32[896,4864]{1,0:T(8,128)S(1)} %get-tuple-element.11.m_ref), custom_call_target="tpu_custom_call" | custom-call | tf_op jit(solution)/shard_map/factor/pallas_call | solution.py:330
  53.7 9.9 %new_error.1 = (f32[896,4864]{1,0:T(8,128)}, f32[8,896]{1,0:T(8,128)}, f32[8,4864]{1,0:T(8,128)}) custom-call(f32[8,896]{1,0:T(8,128)S(1)} %get-tuple-element.12.pt_ref, f32[8,4864]{1,0:T(8,128)S(1)} %get-tuple-element.13.qn_ref, f32[896,4864]{1,0:T(8,128)S(1)} %get-tuple-element.11.m_ref), custom_call_target="tpu_custom_call" | custom-call | tf_op jit(solution)/shard_map/new_error/pallas_call | solution.py:354

commit v4 on v3

--- a/solution.py
+++ b/solution.py
@@ -17,16 +17,18 @@
 N_CHUNK = D_OUT // CHUNK
 HALF = D_OUT // 2
 SIDE = D_IN // 2
+BANDS = ((0, 32), (32, 96), (128, 128), (256, 128), (384, 128), (512, 128), (640, 128), (768, 128))
+SHARES = ((0, 512), (512, 512), (1024, 512), (1536, 512), (2048, 384))
 SLAB = 64
 SLABS = SIDE // SLAB
 PADDED = 4 * RANK
-AHEAD = 6
+AHEAD = 18
 MESH = pl.DeviceIdType.MESH
 C0 = 0.7978845608028654
 C1 = 0.044715
 VMEM_MERGE = 44 * 1024 * 1024
 VMEM_FACTOR = 20 * 1024 * 1024
-VMEM_ERROR = 20 * 1024 * 1024
+VMEM_ERROR = 24 * 1024 * 1024
 
 
 def split3(x):
@@ -164,16 +166,11 @@
             gelu_slab(0, 2 * b + 1)
         start(AHEAD)
         step(0, 0, True, True, False, False)
-        start(AHEAD + 1)
         step(1, 1, True, True, True, False)
 
         def pair(i, carry):
             for par in range(2):
                 c = 2 * i + par
-
-                @pl.when(c + AHEAD < N_CHUNK)
-                def _():
-                    start(c + AHEAD)
 
                 @pl.when(c + 1 < N_CHUNK)
                 def _():
@@ -202,8 +199,8 @@
         tuple(tuple(acc(q, PADDED) for _ in range(2)) for q in range(2)))
 
 
-def factor_kernel(p_ref, m_ref, pt_ref, qn_ref, p_all, pc0, pc1, q_part, q_pair, q_all,
-                  sem_ps, sem_pr, sem_q1, sem_q2s, sem_q2r, sem_q3):
+def factor_kernel(p_ref, m_ref, pt_ref, qn_ref, p_all, p3_v, pc0, pc1, q_mine, q_part, q_pair, q_all,
+                  sem_ps, sem_pr, sem_d, sem_is, sem_ir, sem_f):
     me = lax.axis_index('data')
     core = lax.rem(me, 2)
     chip = me // 2
@@ -221,8 +218,64 @@
             src_ref=p_ref, dst_ref=p_all.at[me], send_sem=sem_ps.at[d], recv_sem=sem_pr.at[d],
             device_id=(lax.rem(me + d, GROUP),), device_id_type=MESH)
 
+    work = []
+    for g, (off, width) in enumerate(SHARES):
+        for mine in range(2):
+            work.append((g, mine, off, width))
+
+    def split_block(n):
+        _, mine, off, width = work[n]
+        half = core if mine else 1 - core
+        cols = pl.ds(pl.multiple_of(half * HALF + off, LANES), width)
+        for r in range(0, D_IN, SLAB):
+            rows = pl.ds(r, SLAB)
+            for t, piece in enumerate(split3(m_ref[rows, cols])):
+                for b in range(width // LANES):
+                    pieces[n % 2][t, b, rows, :] = piece[:, b * LANES:(b + 1) * LANES]
+
+    def rank_block(n):
+        _, mine, off, width = work[n]
+        p3 = jnp.concatenate([p3_v[b] for b in range(D_IN // LANES)], axis=1)
+        acc = None
+        for t in range(3):
+            tile = jnp.concatenate([pieces[n % 2][t, b] for b in range(width // LANES)], axis=1)
+            part = jnp.dot(p3, tile, preferred_element_type=F32)
+            acc = part if acc is None else acc + part
+        dst = q_mine if mine else q_part
+        dst[:, off:off + width] = acc[0:8] + acc[8:16] + acc[16:24]
+
+    def to_mate(g):
+        cols = pl.ds(*SHARES[g])
+        return pltpu.make_async_remote_copy(
+            src_ref=q_part.at[:, cols], dst_ref=q_pair.at[:, cols], send_sem=sem_d.at[0, g],
+            recv_sem=sem_d.at[1, g], device_id=(mate,), device_id_type=MESH)
+
+    def to_chip(g, d):
+        view = q_all.at[chip, :, pl.ds(*SHARES[g])]
+        return pltpu.make_async_remote_copy(
+            src_ref=view, dst_ref=view, send_sem=sem_is.at[d, g], recv_sem=sem_ir.at[d, g],
+            device_id=(lax.rem(me + 2 * d, GROUP),), device_id_type=MESH)
+
+    def my_cols(g):
+        off, width = SHARES[g]
+        return pl.ds(pl.multiple_of(core * HALF + off, LANES), width)
+
+    def final(g):
+        view = qn_ref.at[:, my_cols(g)]
+        return pltpu.make_async_remote_copy(
+            src_ref=view, dst_ref=view, send_sem=sem_f.at[0, g], recv_sem=sem_f.at[1, g],
+            device_id=(mate,), device_id_type=MESH)
+
+    def share_chip_sum(g):
+        cols = pl.ds(*SHARES[g])
+        to_mate(g).wait()
+        q_all[chip, :, cols] = q_mine[:, cols] + q_pair[:, cols]
+        for d in (2, 1, 3):
+            to_chip(g, d).start()
+
     for d in range(1, GROUP):
         p_copy(d).start()
+    split_block(0)
     for d in range(1, GROUP):
         p_copy(d).wait()
     p_sum = p_all[0]
@@ -230,77 +283,52 @@
         p_sum = p_sum + p_all[d]
     p_t = orthonormal_rows(p_sum)
     pt_ref[...] = p_t
-    p3 = stacked(split3(p_t))
-
-    def split_block(half, off, width, par):
-        cols = pl.ds(pl.multiple_of(half * HALF + off, LANES), width)
-        for r in range(0, D_IN, SLAB):
-            rows = pl.ds(r, SLAB)
-            for t, piece in enumerate(split3(m_ref[rows, cols])):
-                for b in range(width // LANES):
-                    pieces[par][t, b, rows, :] = piece[:, b * LANES:(b + 1) * LANES]
-
-    def q_block(width, par):
-        acc = None
-        for t in range(3):
-            tile = jnp.concatenate([pieces[par][t, b] for b in range(width // LANES)], axis=1)
-            part = jnp.dot(p3, tile, preferred_element_type=F32)
-            acc = part if acc is None else acc + part
-        return acc[0:8] + acc[8:16] + acc[16:24]
-
-    blocks = [(off, min(CHUNK, HALF - off)) for off in range(0, HALF, CHUNK)]
-    work = [(1 - core, off, width) for off, width in blocks] + [(core, off, width) for off, width in blocks]
-    to_mate = pltpu.make_async_remote_copy(
-        src_ref=q_part, dst_ref=q_pair, send_sem=sem_q1.at[0], recv_sem=sem_q1.at[1],
-        device_id=(mate,), device_id_type=MESH)
-    own = []
-    split_block(*work[0], 0)
-    for n, (half, off, width) in enumerate(work):
-        if n + 1 < len(work):
-            split_block(*work[n + 1], (n + 1) % 2)
-        val = q_block(width, n % 2)
-        if n < len(blocks):
-            q_part[:, off:off + width] = val
-            if n == len(blocks) - 1:
-                to_mate.start()
-        else:
-            own.append(val)
-    to_mate.wait()
-    for (off, width), val in zip(blocks, own):
-        q_all[chip, :, off:off + width] = val + q_pair[:, off:off + width]
-
-    def q_copy(d):
-        return pltpu.make_async_remote_copy(
-            src_ref=q_all.at[chip], dst_ref=q_all.at[chip], send_sem=sem_q2s.at[d], recv_sem=sem_q2r.at[d],
-            device_id=(lax.rem(me + 2 * d, GROUP),), device_id_type=MESH)
-
-    for d in range(1, 4):
-        q_copy(d).start()
-    for d in range(1, 4):
-        q_copy(d).wait()
-    my_half = pl.ds(pl.multiple_of(core * HALF, LANES), HALF)
-    qn_ref[:, my_half] = (q_all[0] + q_all[1] + q_all[2] + q_all[3]) * (1.0 / GROUP)
-    done = pltpu.make_async_remote_copy(
-        src_ref=qn_ref.at[:, my_half], dst_ref=qn_ref.at[:, my_half], send_sem=sem_q3.at[0],
-        recv_sem=sem_q3.at[1], device_id=(mate,), device_id_type=MESH)
-    done.start()
-    done.wait()
-
-
-def error_kernel(pt_ref, qn_ref, m_ref, e_ref, po_ref, qo_ref, left_ref, right_ref):
-    @pl.when(pl.program_id(0) == 0)
-    def _():
-        po_ref[...] = pt_ref[...]
-        qo_ref[...] = qn_ref[...]
-        ph, pm, pl_ = split3(pt_ref[...])
-        qh, qm, ql = split3(qn_ref[...])
-        left_ref[...] = stacked((ph, ph, ph, pm, pm, pl_)).T
-        right_ref[...] = stacked((qh, qm, ql, qh, qm, qh))
-
-    n = e_ref.shape[0]
-    rows = pl.ds(pl.multiple_of(pl.program_id(0) * n, 16), n)
-    est = jnp.dot(left_ref[rows, :], right_ref[...], preferred_element_type=F32)
-    e_ref[...] = m_ref[rows, :] - est
+    p3 = stacked(split3(p_t) + (jnp.zeros_like(p_t),))
+    for b in range(D_IN // LANES):
+        p3_v[b] = p3[:, b * LANES:(b + 1) * LANES]
+
+    for n, (g, mine, off, width) in enumerate(work):
+        @pl.when(me > -1 - n)
+        def _(n=n):
+            if n + 1 < len(work):
+                split_block(n + 1)
+            rank_block(n)
+
+        last = n + 1 == len(work) or work[n + 1][:2] != (g, mine)
+        if last and not mine:
+            to_mate(g).start()
+        if last and mine:
+            if g:
+                share_chip_sum(g - 1)
+    share_chip_sum(len(SHARES) - 1)
+    for g in range(len(SHARES)):
+        cols = pl.ds(*SHARES[g])
+        for d in range(1, 4):
+            to_chip(g, d).wait()
+        qn_ref[:, my_cols(g)] = (q_all[0, :, cols] + q_all[1, :, cols] + q_all[2, :, cols] + q_all[3, :, cols]) * (1.0 / GROUP)
+        final(g).start()
+    for g in range(len(SHARES)):
+        final(g).wait()
+
+
+def error_kernel(pt_ref, qn_ref, m_ref, e_hbm, po_ref, qo_ref, e_v, left_ref, right_ref, sem):
+    po_ref[...] = pt_ref[...]
+    qo_ref[...] = qn_ref[...]
+    ph, pm, pl_ = split3(pt_ref[...])
+    qh, qm, ql = split3(qn_ref[...])
+    left_ref[...] = stacked((ph, ph, ph, pm, pm, pl_)).T
+    right_ref[...] = stacked((qh, qm, ql, qh, qm, qh))
+
+    def copy(n):
+        rows = pl.ds(*BANDS[n])
+        return pltpu.make_async_copy(e_v.at[rows, :], e_hbm.at[rows, :], sem.at[n])
+
+    for n, band in enumerate(BANDS):
+        rows = pl.ds(*band)
+        e_v[rows, :] = m_ref[rows, :] - jnp.dot(left_ref[rows, :], right_ref[...], preferred_element_type=F32)
+        copy(n).start()
+    for n in range(len(BANDS)):
+        copy(n).wait()
 
 
 def per_device(act_in, pre_act, grad_out, q_init, err_mem):
@@ -334,32 +362,32 @@
         out_specs=(vm, vm),
         scratch_shapes=[
             pltpu.VMEM((GROUP, RANK, D_IN), F32),
-            pltpu.VMEM((3, 2, D_IN, LANES), BF16),
-            pltpu.VMEM((3, 2, D_IN, LANES), BF16),
+            pltpu.VMEM((D_IN // LANES, PADDED, LANES), BF16),
+            pltpu.VMEM((3, 4, D_IN, LANES), BF16),
+            pltpu.VMEM((3, 4, D_IN, LANES), BF16),
+            pltpu.VMEM((RANK, HALF), F32),
             pltpu.VMEM((RANK, HALF), F32),
             pltpu.VMEM((RANK, HALF), F32),
             pltpu.VMEM((4, RANK, HALF), F32),
             pltpu.SemaphoreType.DMA((GROUP,)),
             pltpu.SemaphoreType.DMA((GROUP,)),
-            pltpu.SemaphoreType.DMA((2,)),
-            pltpu.SemaphoreType.DMA((4,)),
-            pltpu.SemaphoreType.DMA((4,)),
-            pltpu.SemaphoreType.DMA((2,)),
+            pltpu.SemaphoreType.DMA((2, len(SHARES))),
+            pltpu.SemaphoreType.DMA((4, len(SHARES))),
+            pltpu.SemaphoreType.DMA((4, len(SHARES))),
+            pltpu.SemaphoreType.DMA((2, len(SHARES))),
         ],
         compiler_params=pltpu.CompilerParams(
             collective_id=0, has_side_effects=True, vmem_limit_bytes=VMEM_FACTOR),
         name='factor',
     )(p_part, merged)
-    bh = 64
     err_new, p_o, qn_o = pl.pallas_call(
         error_kernel,
-        grid=(D_IN // bh,),
         out_shape=(jax.ShapeDtypeStruct((D_IN, D_OUT), F32), jax.ShapeDtypeStruct((RANK, D_IN), F32),
                    jax.ShapeDtypeStruct((RANK, D_OUT), F32)),
         in_specs=[vm, vm, vm],
-        out_specs=(pl.BlockSpec((bh, D_OUT), lambda i: (i, 0)), pl.BlockSpec((RANK, D_IN), lambda i: (0, 0)),
-                   pl.BlockSpec((RANK, D_OUT), lambda i: (0, 0))),
-        scratch_shapes=[pltpu.VMEM((D_IN, 6 * RANK), BF16), pltpu.VMEM((6 * RANK, D_OUT), BF16)],
+        out_specs=(anyspec, vm, vm),
+        scratch_shapes=[pltpu.VMEM((D_IN, D_OUT), F32), pltpu.VMEM((D_IN, 6 * RANK), BF16),
+                        pltpu.VMEM((6 * RANK, D_OUT), BF16), pltpu.SemaphoreType.DMA((len(BANDS),))],
         compiler_params=pltpu.CompilerParams(vmem_limit_bytes=VMEM_ERROR),
         name='new_error',
     )(p_t, qn_t, merged)

time: 63.7 us -> 67.6 us (1.061)
  Pallas kernels: 62.9 us -> 66.7 us
    pallas_call x1, Pallas kernels: 30.3 us -> 36.7 us  [per_device(): pl.pallas_call(merge_kernel, out_shape=(pltpu.VMEM((D_IN, D_OUT), F32), p...]
    pallas_call x1, Pallas kernels: 9.93 us -> 7.15 us  [per_device(): pl.pallas_call(error_kernel, out_shape=(jax.ShapeDtypeStruct((D_IN, D_OUT...]
where the time goes in v4:
time: 67.6 us; the launch traced here: 67.5 us
  Pallas kernels  66.7 us (99%)
  between operations  0.81 us (1%)
    pallas_call x1, Pallas kernels, per_device(): pl.pallas_call(merge_kernel, out_shape=(pltpu.VMEM((D_IN, D_OUT), F32), p...  36.7 us
    pallas_call x1, Pallas kernels, per_device(): pl.pallas_call(factor_kernel, out_shape=(pltpu.VMEM((RANK, D_IN), F32), p...  22.8 us
    pallas_call x1, Pallas kernels, per_device(): pl.pallas_call(error_kernel, out_shape=(jax.ShapeDtypeStruct((D_IN, D_OUT...  7.15 us

profile of v4, /device:TPU:0, one launch (start us, length us, event | category | flops | bytes accessed | tf_op | source)
XLA Modules:
  0.0 67.5 jit_solution(11619803903069830797)
XLA Ops:
  0.6 36.7 %merge.1 = (f32[896,4864]{1,0:T(8,128)S(1)}, f32[8,896]{1,0:T(8,128)S(1)}) custom-call(bf16[1024,896]{1,0:T(8,128)(2,1)} %a_hbm.1, bf16[1024,4864]{1,0:T(8,128)(2,1)} %z_hbm.1, bf16[1024,4864]{1,0:T(8,128)(2,1)} %dy_hbm.1, f32[8,4864]{1,0:T(8,128)} %bitcast.6, f32[896,4864]{1,0:T(8,128)} %bitcast.5), custom_call_target="tpu_custom_call" | custom-call | tf_op jit(solution)/shard_map/merge/pallas_call | solution.py:337
  37.4 22.8 %factor.1 = (f32[8,896]{1,0:T(8,128)S(1)}, f32[8,4864]{1,0:T(8,128)S(1)}) custom-call(f32[8,896]{1,0:T(8,128)S(1)} %get-tuple-element.10.p_ref, f32[896,4864]{1,0:T(8,128)S(1)} %get-tuple-element.11.m_ref), custom_call_target="tpu_custom_call" | custom-call | tf_op jit(solution)/shard_map/factor/pallas_call | solution.py:358
  60.2 7.1 %new_error.1 = (f32[896,4864]{1,0:T(8,128)}, f32[8,896]{1,0:T(8,128)}, f32[8,4864]{1,0:T(8,128)}) custom-call(f32[8,896]{1,0:T(8,128)S(1)} %get-tuple-element.12.pt_ref, f32[8,4864]{1,0:T(8,128)S(1)} %get-tuple-element.13.qn_ref, f32[896,4864]{1,0:T(8,128)S(1)} %get-tuple-element.11.m_ref), custom_call_target="tpu_custom_call" | custom-call | tf_op jit(solution)/shard_map/new_error/pallas_call | solution.py:383

commit v5 on v4

--- a/solution.py
+++ b/solution.py
@@ -22,12 +22,12 @@
 SLAB = 64
 SLABS = SIDE // SLAB
 PADDED = 4 * RANK
-AHEAD = 18
+AHEAD = 4
 MESH = pl.DeviceIdType.MESH
 C0 = 0.7978845608028654
 C1 = 0.044715
 VMEM_MERGE = 44 * 1024 * 1024
-VMEM_FACTOR = 20 * 1024 * 1024
+VMEM_FACTOR = 44 * 1024 * 1024
 VMEM_ERROR = 24 * 1024 * 1024
 
 
@@ -82,7 +82,7 @@
 
     def start(c):
         for k in range(3):
-            copy(k, c).start()
+            copy(k, c).start(priority=1)
 
     def gelu_slab(c, j):
         rows = pl.ds(j * SLAB, SLAB)
@@ -150,7 +150,10 @@
 
         load_a = pltpu.make_async_copy(a_hbm, a_v, sem_a)
         load_a.start()
-        for c in range(AHEAD):
+        copy(0, 0).start()
+        copy(1, 0).start()
+        copy(2, 0).start(priority=1)
+        for c in range(1, AHEAD):
             start(c)
         qt = qt_ref[...]
         q_all = stacked(split3(qt) + (jnp.zeros_like(qt),))
@@ -166,11 +169,16 @@
             gelu_slab(0, 2 * b + 1)
         start(AHEAD)
         step(0, 0, True, True, False, False)
+        start(AHEAD + 1)
         step(1, 1, True, True, True, False)
 
         def pair(i, carry):
             for par in range(2):
                 c = 2 * i + par
+
+                @pl.when(c + AHEAD < N_CHUNK)
+                def _():
+                    start(c + AHEAD)
 
                 @pl.when(c + 1 < N_CHUNK)
                 def _():
@@ -199,23 +207,22 @@
         tuple(tuple(acc(q, PADDED) for _ in range(2)) for q in range(2)))
 
 
-def factor_kernel(p_ref, m_ref, pt_ref, qn_ref, p_all, p3_v, pc0, pc1, q_mine, q_part, q_pair, q_all,
+def factor_kernel(p_in, m_in, pt_ref, qn_ref, m_ref, p_all, p3_v, pc_v, q_mine, q_part, q_pair, q_all,
                   sem_ps, sem_pr, sem_d, sem_is, sem_ir, sem_f):
     me = lax.axis_index('data')
     core = lax.rem(me, 2)
     chip = me // 2
     mate = me + 1 - 2 * core
-    pieces = (pc0, pc1)
 
     barrier = pltpu.get_barrier_semaphore()
     for d in range(1, GROUP):
         pl.semaphore_signal(barrier, inc=1, device_id=(lax.rem(me + d, GROUP),), device_id_type=MESH)
-    p_all[me] = p_ref[...]
+    p_all[me] = pt_ref[...]
     pl.semaphore_wait(barrier, GROUP - 1)
 
     def p_copy(d):
         return pltpu.make_async_remote_copy(
-            src_ref=p_ref, dst_ref=p_all.at[me], send_sem=sem_ps.at[d], recv_sem=sem_pr.at[d],
+            src_ref=pt_ref, dst_ref=p_all.at[me], send_sem=sem_ps.at[d], recv_sem=sem_pr.at[d],
             device_id=(lax.rem(me + d, GROUP),), device_id_type=MESH)
 
     work = []
@@ -223,22 +230,25 @@
         for mine in range(2):
             work.append((g, mine, off, width))
 
-    def split_block(n):
+    def split_all():
+        def one(b, carry):
+            cols = pl.ds(pl.multiple_of(b * LANES, LANES), LANES)
+            for r in range(0, D_IN, SLAB):
+                rows = pl.ds(r, SLAB)
+                for t, piece in enumerate(split3(m_ref[rows, cols])):
+                    pc_v[t, b, rows, :] = piece
+            return carry
+
+        lax.fori_loop(0, D_OUT // LANES, one, 0)
+
+    def rank_block(n):
         _, mine, off, width = work[n]
         half = core if mine else 1 - core
-        cols = pl.ds(pl.multiple_of(half * HALF + off, LANES), width)
-        for r in range(0, D_IN, SLAB):
-            rows = pl.ds(r, SLAB)
-            for t, piece in enumerate(split3(m_ref[rows, cols])):
-                for b in range(width // LANES):
-                    pieces[n % 2][t, b, rows, :] = piece[:, b * LANES:(b + 1) * LANES]
-
-    def rank_block(n):
-        _, mine, off, width = work[n]
+        first = half * (HALF // LANES) + off // LANES
         p3 = jnp.concatenate([p3_v[b] for b in range(D_IN // LANES)], axis=1)
         acc = None
         for t in range(3):
-            tile = jnp.concatenate([pieces[n % 2][t, b] for b in range(width // LANES)], axis=1)
+            tile = jnp.concatenate([pc_v[t, first + b] for b in range(width // LANES)], axis=1)
             part = jnp.dot(p3, tile, preferred_element_type=F32)
             acc = part if acc is None else acc + part
         dst = q_mine if mine else q_part
@@ -275,7 +285,7 @@
 
     for d in range(1, GROUP):
         p_copy(d).start()
-    split_block(0)
+    split_all()
     for d in range(1, GROUP):
         p_copy(d).wait()
     p_sum = p_all[0]
@@ -288,12 +298,7 @@
         p3_v[b] = p3[:, b * LANES:(b + 1) * LANES]
 
     for n, (g, mine, off, width) in enumerate(work):
-        @pl.when(me > -1 - n)
-        def _(n=n):
-            if n + 1 < len(work):
-                split_block(n + 1)
-            rank_block(n)
-
+        rank_block(n)
         last = n + 1 == len(work) or work[n + 1][:2] != (g, mine)
         if last and not mine:
             to_mate(g).start()
@@ -355,16 +360,16 @@
         compiler_params=pltpu.CompilerParams(vmem_limit_bytes=VMEM_MERGE),
         name='merge',
     )(act_in, pre_act, grad_out, q_init.T, err_mem.reshape(D_IN, D_OUT))
-    p_t, qn_t = pl.pallas_call(
+    p_t, qn_t, merged = pl.pallas_call(
         factor_kernel,
-        out_shape=(pltpu.VMEM((RANK, D_IN), F32), pltpu.VMEM((RANK, D_OUT), F32)),
+        out_shape=(pltpu.VMEM((RANK, D_IN), F32), pltpu.VMEM((RANK, D_OUT), F32), pltpu.VMEM((D_IN, D_OUT), F32)),
         in_specs=[vm, vm],
-        out_specs=(vm, vm),
+        out_specs=(vm, vm, vm),
+        input_output_aliases={0: 0, 1: 2},
         scratch_shapes=[
             pltpu.VMEM((GROUP, RANK, D_IN), F32),
             pltpu.VMEM((D_IN // LANES, PADDED, LANES), BF16),
-            pltpu.VMEM((3, 4, D_IN, LANES), BF16),
-            pltpu.VMEM((3, 4, D_IN, LANES), BF16),
+            pltpu.VMEM((3, D_OUT // LANES, D_IN, LANES), BF16),
             pltpu.VMEM((RANK, HALF), F32),
             pltpu.VMEM((RANK, HALF), F32),
             pltpu.VMEM((RANK, HALF), F32),

time: 67.6 us -> 56 us (0.83)
  Pallas kernels: 66.7 us -> 55.1 us
    pallas_call x1, Pallas kernels: 36.7 us -> 27.3 us  [per_device(): pl.pallas_call(merge_kernel, out_shape=(pltpu.VMEM((D_IN, D_OUT), F32), p...]
    pallas_call x1, Pallas kernels: 22.8 us -> 20.6 us  [per_device(): pl.pallas_call(factor_kernel, out_shape=(pltpu.VMEM((RANK, D_IN), F32), p...]
where the time goes in v5:
time: 56 us; the launch traced here: 55.9 us
  Pallas kernels  55.1 us (98%)
  between operations  0.81 us (1%)
    pallas_call x1, Pallas kernels, per_device(): pl.pallas_call(merge_kernel, out_shape=(pltpu.VMEM((D_IN, D_OUT), F32), p...  27.3 us
    pallas_call x1, Pallas kernels, per_device(): pl.pallas_call(factor_kernel, out_shape=(pltpu.VMEM((RANK, D_IN), F32), p...  20.6 us
    pallas_call x1, Pallas kernels, per_device(): pl.pallas_call(error_kernel, out_shape=(jax.ShapeDtypeStruct((D_IN, D_OUT...  7.15 us

profile of v5, /device:TPU:0, one launch (start us, length us, event | category | flops | bytes accessed | tf_op | source)
XLA Modules:
  0.0 55.9 jit_solution(3431377173893749379)
XLA Ops:
  0.6 27.3 %merge.1 = (f32[896,4864]{1,0:T(8,128)S(1)}, f32[8,896]{1,0:T(8,128)S(1)}) custom-call(bf16[1024,896]{1,0:T(8,128)(2,1)} %a_hbm.1, bf16[1024,4864]{1,0:T(8,128)(2,1)} %z_hbm.1, bf16[1024,4864]{1,0:T(8,128)(2,1)} %dy_hbm.1, f32[8,4864]{1,0:T(8,128)} %bitcast.6, f32[896,4864]{1,0:T(8,128)} %bitcast.5), custom_call_target="tpu_custom_call" | custom-call | tf_op jit(solution)/shard_map/merge/pallas_call | solution.py:342
  28.0 20.6 %factor.1 = (f32[8,896]{1,0:T(8,128)S(1)}, f32[8,4864]{1,0:T(8,128)S(1)}, f32[896,4864]{1,0:T(8,128)S(1)}) custom-call(f32[8,896]{1,0:T(8,128)S(1)} %get-tuple-element.11.p_in, f32[896,4864]{1,0:T(8,128)S(1)} %get-tuple-element.12.m_in), custom_call_target="tpu_custom_call", output_to_operand_aliasing={{0}: (0, {}), {2}: (1, {})} | custom-call | tf_op jit(solution)/shard_map/factor/pallas_call | solution.py:363
  48.6 7.2 %new_error.1 = (f32[896,4864]{1,0:T(8,128)}, f32[8,896]{1,0:T(8,128)}, f32[8,4864]{1,0:T(8,128)}) custom-call(f32[8,896]{1,0:T(8,128)S(1)} %get-tuple-element.13.pt_ref, f32[8,4864]{1,0:T(8,128)S(1)} %get-tuple-element.14.qn_ref, f32[896,4864]{1,0:T(8,128)S(1)} %get-tuple-element.15.m_ref), custom_call_target="tpu_custom_call" | custom-call | tf_op jit(solution)/shard_map/new_error/pallas_call | solution.py:388

commit v6 on v5

--- a/solution.py
+++ b/solution.py
@@ -17,7 +17,6 @@
 N_CHUNK = D_OUT // CHUNK
 HALF = D_OUT // 2
 SIDE = D_IN // 2
-BANDS = ((0, 32), (32, 96), (128, 128), (256, 128), (384, 128), (512, 128), (640, 128), (768, 128))
 SHARES = ((0, 512), (512, 512), (1024, 512), (1536, 512), (2048, 384))
 SLAB = 64
 SLABS = SIDE // SLAB
@@ -78,7 +77,7 @@
 
     def copy(k, c):
         src, dst = ((z_hbm, z_v), (dy_hbm, dy_v), (e_hbm, m_ref))[k]
-        return pltpu.make_async_copy(src.at[:, cols_of(c)], dst.at[:, cols_of(c)], sem_in.at[k, c])
+        return pltpu.make_async_copy(src.at[:, cols_of(c)], dst.at[c], sem_in.at[k, c])
 
     def start(c):
         for k in range(3):
@@ -86,7 +85,7 @@
 
     def gelu_slab(c, j):
         rows = pl.ds(j * SLAB, SLAB)
-        g = gelu_grad_times(z_v[rows, cols_of(c)], dy_v[rows, cols_of(c)])
+        g = gelu_grad_times(z_v[c, rows, :], dy_v[c, rows, :])
         for b in range(2):
             gs[c_par(c)][b, rows, :] = g[:, b * LANES:(b + 1) * LANES]
 
@@ -98,8 +97,8 @@
     def body_of(accs, p_acc):
         def merge_slab(c, par, q, i):
             rows = pl.ds(q * SIDE + i * SLAB, SLAB)
-            m = pltpu.matmul_pop(accs[par][q][i]) * (1.0 / ROWS) + m_ref[rows, cols_of(c)]
-            m_ref[rows, cols_of(c)] = m
+            m = pltpu.matmul_pop(accs[par][q][i]) * (1.0 / ROWS) + m_ref[c, rows, :]
+            m_ref[c, rows, :] = m
             for t, piece in enumerate(split3(m)):
                 for b in range(2):
                     pieces[par][t, b, rows, :] = piece[:, b * LANES:(b + 1) * LANES]
@@ -217,12 +216,12 @@
     barrier = pltpu.get_barrier_semaphore()
     for d in range(1, GROUP):
         pl.semaphore_signal(barrier, inc=1, device_id=(lax.rem(me + d, GROUP),), device_id_type=MESH)
-    p_all[me] = pt_ref[...]
+    p_all[me] = p_in[...]
     pl.semaphore_wait(barrier, GROUP - 1)
 
     def p_copy(d):
         return pltpu.make_async_remote_copy(
-            src_ref=pt_ref, dst_ref=p_all.at[me], send_sem=sem_ps.at[d], recv_sem=sem_pr.at[d],
+            src_ref=p_in, dst_ref=p_all.at[me], send_sem=sem_ps.at[d], recv_sem=sem_pr.at[d],
             device_id=(lax.rem(me + d, GROUP),), device_id_type=MESH)
 
     work = []
@@ -231,15 +230,15 @@
             work.append((g, mine, off, width))
 
     def split_all():
-        def one(b, carry):
-            cols = pl.ds(pl.multiple_of(b * LANES, LANES), LANES)
+        def one(c, carry):
             for r in range(0, D_IN, SLAB):
                 rows = pl.ds(r, SLAB)
-                for t, piece in enumerate(split3(m_ref[rows, cols])):
-                    pc_v[t, b, rows, :] = piece
+                for t, piece in enumerate(split3(m_in[c, rows, :])):
+                    for b in range(2):
+                        pc_v[t, 2 * c + b, rows, :] = piece[:, b * LANES:(b + 1) * LANES]
             return carry
 
-        lax.fori_loop(0, D_OUT // LANES, one, 0)
+        lax.fori_loop(0, N_CHUNK, one, 0)
 
     def rank_block(n):
         _, mine, off, width = work[n]
@@ -324,16 +323,17 @@
     left_ref[...] = stacked((ph, ph, ph, pm, pm, pl_)).T
     right_ref[...] = stacked((qh, qm, ql, qh, qm, qh))
 
-    def copy(n):
-        rows = pl.ds(*BANDS[n])
-        return pltpu.make_async_copy(e_v.at[rows, :], e_hbm.at[rows, :], sem.at[n])
-
-    for n, band in enumerate(BANDS):
-        rows = pl.ds(*band)
-        e_v[rows, :] = m_ref[rows, :] - jnp.dot(left_ref[rows, :], right_ref[...], preferred_element_type=F32)
-        copy(n).start()
-    for n in range(len(BANDS)):
-        copy(n).wait()
+    def copy(c):
+        return pltpu.make_async_copy(e_v.at[c], e_hbm.at[:, pl.ds(c * CHUNK, CHUNK)], sem.at[c])
+
+    for c in range(N_CHUNK):
+        right = right_ref[:, c * CHUNK:(c + 1) * CHUNK]
+        for r in range(0, D_IN, 224):
+            rows = pl.ds(r, 224)
+            e_v[c, rows, :] = m_ref[c, rows, :] - jnp.dot(left_ref[rows, :], right, preferred_element_type=F32)
+        copy(c).start()
+    for c in range(N_CHUNK):
+        copy(c).wait()
 
 
 def per_device(act_in, pre_act, grad_out, q_init, err_mem):
@@ -341,13 +341,13 @@
     anyspec = pl.BlockSpec(memory_space=pl.ANY)
     merged, p_part = pl.pallas_call(
         merge_kernel,
-        out_shape=(pltpu.VMEM((D_IN, D_OUT), F32), pltpu.VMEM((RANK, D_IN), F32)),
+        out_shape=(pltpu.VMEM((N_CHUNK, D_IN, CHUNK), F32), pltpu.VMEM((RANK, D_IN), F32)),
         in_specs=[anyspec, anyspec, anyspec, vm, anyspec],
         out_specs=(vm, vm),
         scratch_shapes=[
             pltpu.VMEM((ROWS, D_IN), BF16),
-            pltpu.VMEM((ROWS, D_OUT), BF16),
-            pltpu.VMEM((ROWS, D_OUT), BF16),
+            pltpu.VMEM((N_CHUNK, ROWS, CHUNK), BF16),
+            pltpu.VMEM((N_CHUNK, ROWS, CHUNK), BF16),
             pltpu.VMEM((ROWS // LANES, D_IN, LANES), BF16),
             pltpu.VMEM((2 * N_CHUNK, PADDED, LANES), BF16),
             pltpu.VMEM((2, ROWS, LANES), BF16),
@@ -362,7 +362,7 @@
     )(act_in, pre_act, grad_out, q_init.T, err_mem.reshape(D_IN, D_OUT))
     p_t, qn_t, merged = pl.pallas_call(
         factor_kernel,
-        out_shape=(pltpu.VMEM((RANK, D_IN), F32), pltpu.VMEM((RANK, D_OUT), F32), pltpu.VMEM((D_IN, D_OUT), F32)),
+        out_shape=(pltpu.VMEM((RANK, D_IN), F32), pltpu.VMEM((RANK, D_OUT), F32), pltpu.VMEM((N_CHUNK, D_IN, CHUNK), F32)),
         in_specs=[vm, vm],
         out_specs=(vm, vm, vm),
         input_output_aliases={0: 0, 1: 2},
@@ -391,8 +391,8 @@
                    jax.ShapeDtypeStruct((RANK, D_OUT), F32)),
         in_specs=[vm, vm, vm],
         out_specs=(anyspec, vm, vm),
-        scratch_shapes=[pltpu.VMEM((D_IN, D_OUT), F32), pltpu.VMEM((D_IN, 6 * RANK), BF16),
-                        pltpu.VMEM((6 * RANK, D_OUT), BF16), pltpu.SemaphoreType.DMA((len(BANDS),))],
+        scratch_shapes=[pltpu.VMEM((N_CHUNK, D_IN, CHUNK), F32), pltpu.VMEM((D_IN, 6 * RANK), BF16),
+                        pltpu.VMEM((6 * RANK, D_OUT), BF16), pltpu.SemaphoreType.DMA((N_CHUNK,))],
         compiler_params=pltpu.CompilerParams(vmem_limit_bytes=VMEM_ERROR),
         name='new_error',
     )(p_t, qn_t, merged)

time: 56 us -> 55.7 us (level)
  no operation moved by 1% of the time
where the time goes in v6:
time: 55.7 us; the launch traced here: 55.6 us
  Pallas kernels  54.8 us (98%)
  between operations  0.81 us (1%)
    pallas_call x1, Pallas kernels, per_device(): pl.pallas_call(merge_kernel, out_shape=(pltpu.VMEM((N_CHUNK, D_IN, CHUNK)...  27 us
    pallas_call x1, Pallas kernels, per_device(): pl.pallas_call(factor_kernel, out_shape=(pltpu.VMEM((RANK, D_IN), F32), p...  20.6 us
    pallas_call x1, Pallas kernels, per_device(): pl.pallas_call(error_kernel, out_shape=(jax.ShapeDtypeStruct((D_IN, D_OUT...  7.19 us

profile of v6, /device:TPU:0, one launch (start us, length us, event | category | flops | bytes accessed | tf_op | source)
XLA Modules:
  0.0 55.6 jit_solution(8010902384568688223)
XLA Ops:
  0.6 27.0 %merge.1 = (f32[19,896,256]{2,1,0:T(8,128)S(1)}, f32[8,896]{1,0:T(8,128)S(1)}) custom-call(bf16[1024,896]{1,0:T(8,128)(2,1)} %a_hbm.1, bf16[1024,4864]{1,0:T(8,128)(2,1)} %z_hbm.1, bf16[1024,4864]{1,0:T(8,128)(2,1)} %dy_hbm.1, f32[8,4864]{1,0:T(8,128)} %bitcast.6, f32[896,4864]{1,0:T(8,128)} %bitcast.5), custom_call_target="tpu_custom_call" | custom-call | tf_op jit(solution)/shard_map/merge/pallas_call | solution.py:342
  27.7 20.6 %factor.1 = (f32[8,896]{1,0:T(8,128)S(1)}, f32[8,4864]{1,0:T(8,128)S(1)}, f32[19,896,256]{2,1,0:T(8,128)S(1)}) custom-call(f32[8,896]{1,0:T(8,128)S(1)} %get-tuple-element.11.p_in, f32[19,896,256]{2,1,0:T(8,128)S(1)} %get-tuple-element.12.m_in), custom_call_target="tpu_custom_call", output_to_operand_aliasing={{0}: (0, {}), {2}: (1, {})} | custom-call | tf_op jit(solution)/shard_map/factor/pallas_call | solution.py:363
  48.2 7.2 %new_error.1 = (f32[896,4864]{1,0:T(8,128)}, f32[8,896]{1,0:T(8,128)}, f32[8,4864]{1,0:T(8,128)}) custom-call(f32[8,896]{1,0:T(8,128)S(1)} %get-tuple-element.13.pt_ref, f32[8,4864]{1,0:T(8,128)S(1)} %get-tuple-element.14.qn_ref, f32[19,896,256]{2,1,0:T(8,128)S(1)} %get-tuple-element.15.m_ref), custom_call_target="tpu_custom_call" | custom-call | tf_op jit(solution)/shard_map/new_error/pallas_call | solution.py:388

commit v7 on v6

--- a/solution.py
+++ b/solution.py
@@ -17,7 +17,8 @@
 N_CHUNK = D_OUT // CHUNK
 HALF = D_OUT // 2
 SIDE = D_IN // 2
-SHARES = ((0, 512), (512, 512), (1024, 512), (1536, 512), (2048, 384))
+SHARES = ((0, 512), (512, 512), (1024, 512), (1536, 512), (2048, 256), (2304, 128))
+LAST = len(SHARES) - 1
 SLAB = 64
 SLABS = SIDE // SLAB
 PADDED = 4 * RANK
@@ -67,8 +68,8 @@
     return jnp.concatenate([ref[first, rows, :], ref[first + 1, rows, :]], axis=1)
 
 
-def merge_kernel(a_hbm, z_hbm, dy_hbm, qt_ref, e_hbm, m_ref, p_ref,
-                 a_v, z_v, dy_v, at_ref, q3_v, g0, g1, pc0, pc1, sem_in, sem_a):
+def merge_kernel(a_hbm, z_hbm, dy_hbm, qt_hbm, e_hbm, m_ref, p_ref,
+                 a_v, z_v, dy_v, qt_v, at_ref, q3_v, g0, g1, pc0, pc1, sem_in, sem_a, sem_q):
     gs = (g0, g1)
     pieces = (pc0, pc1)
 
@@ -151,13 +152,11 @@
         load_a.start()
         copy(0, 0).start()
         copy(1, 0).start()
+        load_q = pltpu.make_async_copy(qt_hbm, qt_v, sem_q)
+        load_q.start(priority=1)
         copy(2, 0).start(priority=1)
         for c in range(1, AHEAD):
             start(c)
-        qt = qt_ref[...]
-        q_all = stacked(split3(qt) + (jnp.zeros_like(qt),))
-        for b in range(2 * N_CHUNK):
-            q3_v[b] = q_all[:, b * LANES:(b + 1) * LANES]
         load_a.wait()
         copy(0, 0).wait()
         copy(1, 0).wait()
@@ -167,6 +166,11 @@
             gelu_slab(0, 2 * b)
             gelu_slab(0, 2 * b + 1)
         start(AHEAD)
+        load_q.wait()
+        qt = qt_v[...]
+        q_all = stacked(split3(qt) + (jnp.zeros_like(qt),))
+        for b in range(2 * N_CHUNK):
+            q3_v[b] = q_all[:, b * LANES:(b + 1) * LANES]
         step(0, 0, True, True, False, False)
         start(AHEAD + 1)
         step(1, 1, True, True, True, False)
@@ -206,8 +210,8 @@
         tuple(tuple(acc(q, PADDED) for _ in range(2)) for q in range(2)))
 
 
-def factor_kernel(p_in, m_in, pt_ref, qn_ref, m_ref, p_all, p3_v, pc_v, q_mine, q_part, q_pair, q_all,
-                  sem_ps, sem_pr, sem_d, sem_is, sem_ir, sem_f):
+def factor_kernel(p_in, m_in, pt_ref, qn_ref, m_ref, p_all, p3_v, pc_v, q_mine, q_part, q_pair, q_all, q_other,
+                  sem_ps, sem_pr, sem_d, sem_is, sem_ir, sem_f, sem_o):
     me = lax.axis_index('data')
     core = lax.rem(me, 2)
     chip = me // 2
@@ -224,10 +228,10 @@
             src_ref=p_in, dst_ref=p_all.at[me], send_sem=sem_ps.at[d], recv_sem=sem_pr.at[d],
             device_id=(lax.rem(me + d, GROUP),), device_id_type=MESH)
 
-    work = []
-    for g, (off, width) in enumerate(SHARES):
-        for mine in range(2):
-            work.append((g, mine, off, width))
+    work = [(0, 0)]
+    for g in range(LAST):
+        work += [(g + 1, 0), (g, 1)]
+    work.append((LAST, 1))
 
     def split_all():
         def one(c, carry):
@@ -241,7 +245,8 @@
         lax.fori_loop(0, N_CHUNK, one, 0)
 
     def rank_block(n):
-        _, mine, off, width = work[n]
+        g, mine = work[n]
+        off, width = SHARES[g]
         half = core if mine else 1 - core
         first = half * (HALF // LANES) + off // LANES
         p3 = jnp.concatenate([p3_v[b] for b in range(D_IN // LANES)], axis=1)
@@ -275,12 +280,26 @@
             src_ref=view, dst_ref=view, send_sem=sem_f.at[0, g], recv_sem=sem_f.at[1, g],
             device_id=(mate,), device_id_type=MESH)
 
+    def to_other(d):
+        return pltpu.make_async_remote_copy(
+            src_ref=q_all.at[chip, :, pl.ds(*SHARES[LAST])], dst_ref=q_other.at[chip], send_sem=sem_o.at[0, d],
+            recv_sem=sem_o.at[1, d], device_id=(lax.rem(mate + 2 * d, GROUP),), device_id_type=MESH)
+
+    mate_cols = pl.ds(pl.multiple_of((1 - core) * HALF + SHARES[LAST][0], LANES), SHARES[LAST][1])
+
+    def mean_of(parts):
+        return (parts[0] + parts[1] + parts[2] + parts[3]) * (1.0 / GROUP)
+
     def share_chip_sum(g):
         cols = pl.ds(*SHARES[g])
         to_mate(g).wait()
         q_all[chip, :, cols] = q_mine[:, cols] + q_pair[:, cols]
         for d in (2, 1, 3):
             to_chip(g, d).start()
+            if g == LAST:
+                to_other(d).start()
+        if g == LAST:
+            to_other(0).start()
 
     for d in range(1, GROUP):
         p_copy(d).start()
@@ -296,28 +315,31 @@
     for b in range(D_IN // LANES):
         p3_v[b] = p3[:, b * LANES:(b + 1) * LANES]
 
-    for n, (g, mine, off, width) in enumerate(work):
+    for n, (g, mine) in enumerate(work):
         rank_block(n)
-        last = n + 1 == len(work) or work[n + 1][:2] != (g, mine)
-        if last and not mine:
+        if mine:
+            share_chip_sum(g)
+        else:
             to_mate(g).start()
-        if last and mine:
-            if g:
-                share_chip_sum(g - 1)
-    share_chip_sum(len(SHARES) - 1)
     for g in range(len(SHARES)):
         cols = pl.ds(*SHARES[g])
         for d in range(1, 4):
             to_chip(g, d).wait()
-        qn_ref[:, my_cols(g)] = (q_all[0, :, cols] + q_all[1, :, cols] + q_all[2, :, cols] + q_all[3, :, cols]) * (1.0 / GROUP)
-        final(g).start()
-    for g in range(len(SHARES)):
+        qn_ref[:, my_cols(g)] = mean_of([q_all[k, :, cols] for k in range(4)])
+        if g < LAST:
+            final(g).start()
+    for d in range(4):
+        to_other(d).wait()
+    qn_ref[:, mate_cols] = mean_of([q_other[k] for k in range(4)])
+    for g in range(LAST):
         final(g).wait()
 
 
-def error_kernel(pt_ref, qn_ref, m_ref, e_hbm, po_ref, qo_ref, e_v, left_ref, right_ref, sem):
-    po_ref[...] = pt_ref[...]
-    qo_ref[...] = qn_ref[...]
+def error_kernel(pt_ref, qn_ref, m_ref, e_hbm, po_hbm, qo_hbm, e_v, left_ref, right_ref, sem):
+    factors = (pltpu.make_async_copy(pt_ref, po_hbm, sem.at[N_CHUNK]),
+               pltpu.make_async_copy(qn_ref, qo_hbm, sem.at[N_CHUNK + 1]))
+    for move in factors:
+        move.start()
     ph, pm, pl_ = split3(pt_ref[...])
     qh, qm, ql = split3(qn_ref[...])
     left_ref[...] = stacked((ph, ph, ph, pm, pm, pl_)).T
@@ -332,6 +354,8 @@
             rows = pl.ds(r, 224)
             e_v[c, rows, :] = m_ref[c, rows, :] - jnp.dot(left_ref[rows, :], right, preferred_element_type=F32)
         copy(c).start()
+    for move in factors:
+        move.wait()
     for c in range(N_CHUNK):
         copy(c).wait()
 
@@ -342,12 +366,13 @@
     merged, p_part = pl.pallas_call(
         merge_kernel,
         out_shape=(pltpu.VMEM((N_CHUNK, D_IN, CHUNK), F32), pltpu.VMEM((RANK, D_IN), F32)),
-        in_specs=[anyspec, anyspec, anyspec, vm, anyspec],
+        in_specs=[anyspec, anyspec, anyspec, anyspec, anyspec],
         out_specs=(vm, vm),
         scratch_shapes=[
             pltpu.VMEM((ROWS, D_IN), BF16),
             pltpu.VMEM((N_CHUNK, ROWS, CHUNK), BF16),
             pltpu.VMEM((N_CHUNK, ROWS, CHUNK), BF16),
+            pltpu.VMEM((RANK, D_OUT), F32),
             pltpu.VMEM((ROWS // LANES, D_IN, LANES), BF16),
             pltpu.VMEM((2 * N_CHUNK, PADDED, LANES), BF16),
             pltpu.VMEM((2, ROWS, LANES), BF16),
@@ -355,6 +380,7 @@
             pltpu.VMEM((3, 2, D_IN, LANES), BF16),
             pltpu.VMEM((3, 2, D_IN, LANES), BF16),
             pltpu.SemaphoreType.DMA((3, N_CHUNK)),
+            pltpu.SemaphoreType.DMA,
             pltpu.SemaphoreType.DMA,
         ],
         compiler_params=pltpu.CompilerParams(vmem_limit_bytes=VMEM_MERGE),
@@ -374,12 +400,14 @@
             pltpu.VMEM((RANK, HALF), F32),
             pltpu.VMEM((RANK, HALF), F32),
             pltpu.VMEM((4, RANK, HALF), F32),
+            pltpu.VMEM((4, RANK, SHARES[LAST][1]), F32),
             pltpu.SemaphoreType.DMA((GROUP,)),
             pltpu.SemaphoreType.DMA((GROUP,)),
             pltpu.SemaphoreType.DMA((2, len(SHARES))),
             pltpu.SemaphoreType.DMA((4, len(SHARES))),
             pltpu.SemaphoreType.DMA((4, len(SHARES))),
             pltpu.SemaphoreType.DMA((2, len(SHARES))),
+            pltpu.SemaphoreType.DMA((2, 4)),
         ],
         compiler_params=pltpu.CompilerParams(
             collective_id=0, has_side_effects=True, vmem_limit_bytes=VMEM_FACTOR),
@@ -390,9 +418,9 @@
         out_shape=(jax.ShapeDtypeStruct((D_IN, D_OUT), F32), jax.ShapeDtypeStruct((RANK, D_IN), F32),
                    jax.ShapeDtypeStruct((RANK, D_OUT), F32)),
         in_specs=[vm, vm, vm],
-        out_specs=(anyspec, vm, vm),
+        out_specs=(anyspec, anyspec, anyspec),
         scratch_shapes=[pltpu.VMEM((N_CHUNK, D_IN, CHUNK), F32), pltpu.VMEM((D_IN, 6 * RANK), BF16),
-                        pltpu.VMEM((6 * RANK, D_OUT), BF16), pltpu.SemaphoreType.DMA((N_CHUNK,))],
+                        pltpu.VMEM((6 * RANK, D_OUT), BF16), pltpu.SemaphoreType.DMA((N_CHUNK + 2,))],
         compiler_params=pltpu.CompilerParams(vmem_limit_bytes=VMEM_ERROR),
         name='new_error',
     )(p_t, qn_t, merged)

time: 55.7 us -> 55.3 us (level)
    pallas_call x1, Pallas kernels: 7.19 us -> 6.53 us  [per_device(): pl.pallas_call(error_kernel, out_shape=(jax.ShapeDtypeStruct((D_IN, D_OUT...]
where the time goes in v7:
time: 55.3 us
  Pallas kernels  54.4 us (98%)
  between operations  0.81 us (1%)
    pallas_call x1, Pallas kernels, per_device(): pl.pallas_call(merge_kernel, out_shape=(pltpu.VMEM((N_CHUNK, D_IN, CHUNK)...  27 us
    pallas_call x1, Pallas kernels, per_device(): pl.pallas_call(factor_kernel, out_shape=(pltpu.VMEM((RANK, D_IN), F32), p...  20.9 us
    pallas_call x1, Pallas kernels, per_device(): pl.pallas_call(error_kernel, out_shape=(jax.ShapeDtypeStruct((D_IN, D_OUT...  6.53 us

profile of v7, /device:TPU:0, one launch (start us, length us, event | category | flops | bytes accessed | tf_op | source)
XLA Modules:
  0.0 55.3 jit_solution(695795752057473086)
XLA Ops:
  0.6 27.0 %merge.1 = (f32[19,896,256]{2,1,0:T(8,128)S(1)}, f32[8,896]{1,0:T(8,128)S(1)}) custom-call(bf16[1024,896]{1,0:T(8,128)(2,1)} %a_hbm.1, bf16[1024,4864]{1,0:T(8,128)(2,1)} %z_hbm.1, bf16[1024,4864]{1,0:T(8,128)(2,1)} %dy_hbm.1, f32[8,4864]{1,0:T(8,128)} %bitcast.6, f32[896,4864]{1,0:T(8,128)} %bitcast.5), custom_call_target="tpu_custom_call" | custom-call | tf_op jit(solution)/shard_map/merge/pallas_call | solution.py:366
  27.6 20.9 %factor.1 = (f32[8,896]{1,0:T(8,128)S(1)}, f32[8,4864]{1,0:T(8,128)S(1)}, f32[19,896,256]{2,1,0:T(8,128)S(1)}) custom-call(f32[8,896]{1,0:T(8,128)S(1)} %get-tuple-element.11.p_in, f32[19,896,256]{2,1,0:T(8,128)S(1)} %get-tuple-element.12.m_in), custom_call_target="tpu_custom_call", output_to_operand_aliasing={{0}: (0, {}), {2}: (1, {})} | custom-call | tf_op jit(solution)/shard_map/factor/pallas_call | solution.py:389
  48.6 6.5 %new_error.1 = (f32[896,4864]{1,0:T(8,128)}, f32[8,896]{1,0:T(8,128)}, f32[8,4864]{1,0:T(8,128)}) custom-call(f32[8,896]{1,0:T(8,128)S(1)} %get-tuple-element.13.pt_ref, f32[8,4864]{1,0:T(8,128)S(1)} %get-tuple-element.14.qn_ref, f32[19,896,256]{2,1,0:T(8,128)S(1)} %get-tuple-element.15.m_ref), custom_call_target="tpu_custom_call" | custom-call | tf_op jit(solution)/shard_map/new_error/pallas_call | solution.py:416

commit v8 on v7

--- a/solution.py
+++ b/solution.py
@@ -17,12 +17,12 @@
 N_CHUNK = D_OUT // CHUNK
 HALF = D_OUT // 2
 SIDE = D_IN // 2
-SHARES = ((0, 512), (512, 512), (1024, 512), (1536, 512), (2048, 256), (2304, 128))
+SHARES = ((0, 512), (512, 512), (1024, 640), (1664, 512), (2176, 256))
 LAST = len(SHARES) - 1
 SLAB = 64
 SLABS = SIDE // SLAB
 PADDED = 4 * RANK
-AHEAD = 4
+PAIRS = N_CHUNK // 2
 MESH = pl.DeviceIdType.MESH
 C0 = 0.7978845608028654
 C1 = 0.044715
@@ -69,24 +69,37 @@
 
 
 def merge_kernel(a_hbm, z_hbm, dy_hbm, qt_hbm, e_hbm, m_ref, p_ref,
-                 a_v, z_v, dy_v, qt_v, at_ref, q3_v, g0, g1, pc0, pc1, sem_in, sem_a, sem_q):
+                 a_v, z0_v, dy0_v, z_v, dy_v, qt_v, at_ref, q3_v, g0, g1, pc0, pc1, sem_e, sem_zy, sem_a, sem_q):
     gs = (g0, g1)
     pieces = (pc0, pc1)
 
     def cols_of(c):
         return pl.ds(c * CHUNK if isinstance(c, int) else pl.multiple_of(c * CHUNK, CHUNK), CHUNK)
 
-    def copy(k, c):
-        src, dst = ((z_hbm, z_v), (dy_hbm, dy_v), (e_hbm, m_ref))[k]
-        return pltpu.make_async_copy(src.at[:, cols_of(c)], dst.at[c], sem_in.at[k, c])
-
-    def start(c):
-        for k in range(3):
-            copy(k, c).start(priority=1)
-
-    def gelu_slab(c, j):
+    def load_e(c):
+        return pltpu.make_async_copy(e_hbm.at[:, cols_of(c)], m_ref.at[c], sem_e.at[c])
+
+    def load_first(k):
+        src, dst = ((z_hbm, z0_v), (dy_hbm, dy0_v))[k]
+        return pltpu.make_async_copy(src.at[:, pl.ds(0, CHUNK)], dst, sem_zy.at[k, PAIRS])
+
+    def load_pair(k, p):
+        src, dst = ((z_hbm, z_v), (dy_hbm, dy_v))[k]
+        first = (2 * p + 1) * CHUNK
+        cols = pl.ds(first if isinstance(first, int) else pl.multiple_of(first, CHUNK), 2 * CHUNK)
+        return pltpu.make_async_copy(src.at[:, cols], dst.at[p], sem_zy.at[k, p])
+
+    def start_pair(p):
+        load_pair(0, p).start(priority=1)
+        load_pair(1, p).start(priority=1)
+
+    def gelu_slab(c, p, half, j):
         rows = pl.ds(j * SLAB, SLAB)
-        g = gelu_grad_times(z_v[c, rows, :], dy_v[c, rows, :])
+        if isinstance(c, int) and c == 0:
+            g = gelu_grad_times(z0_v[rows, :], dy0_v[rows, :])
+        else:
+            cols = pl.ds(half * CHUNK, CHUNK)
+            g = gelu_grad_times(z_v[p, rows, cols], dy_v[p, rows, cols])
         for b in range(2):
             gs[c_par(c)][b, rows, :] = g[:, b * LANES:(b + 1) * LANES]
 
@@ -116,13 +129,14 @@
             pltpu.matmul_push_rhs(tile, staging_register=1, mxu_index=q, transpose=True)
             pltpu.matmul_acc_lhs(p_acc[q][blk], q3, load_staged_rhs=1)
 
-        def step(c, par, gelu, grad, merge, rank):
+        def step(c, p, par, gelu, grad, merge, rank):
             par_box[0] = par
             if gelu:
-                copy(0, c + 1).wait()
-                copy(1, c + 1).wait()
+                if par == 0:
+                    load_pair(0, p).wait()
+                    load_pair(1, p).wait()
             if merge:
-                copy(2, c - 1).wait()
+                load_e(c - 1).wait()
             if rank:
                 q3 = jnp.concatenate([q3_v[2 * (c - 2)], q3_v[2 * (c - 2) + 1]], axis=1)
             tiles = [(blk, t) for blk in range(2) for t in range(3)]
@@ -146,52 +160,60 @@
                 if gelu:
                     for j in range(n_gelu):
                         if j * SLABS // n_gelu == s:
-                            gelu_slab(c + 1, j)
+                            gelu_slab(c + 1, p, par, j)
 
         load_a = pltpu.make_async_copy(a_hbm, a_v, sem_a)
+        load_q = pltpu.make_async_copy(qt_hbm, qt_v, sem_q)
         load_a.start()
-        copy(0, 0).start()
-        copy(1, 0).start()
-        load_q = pltpu.make_async_copy(qt_hbm, qt_v, sem_q)
+        load_first(0).start()
+        load_first(1).start()
+        start_pair(0)
         load_q.start(priority=1)
-        copy(2, 0).start(priority=1)
-        for c in range(1, AHEAD):
-            start(c)
+        load_e(0).start(priority=1)
+        start_pair(1)
+        load_e(1).start(priority=1)
+        load_e(2).start(priority=1)
         load_a.wait()
-        copy(0, 0).wait()
-        copy(1, 0).wait()
+        load_first(0).wait()
+        load_first(1).wait()
         par_box[0] = 1
         for b in range(ROWS // LANES):
             at_ref[b] = a_v[b * LANES:(b + 1) * LANES, :].T
-            gelu_slab(0, 2 * b)
-            gelu_slab(0, 2 * b + 1)
-        start(AHEAD)
+            gelu_slab(0, 0, 0, 2 * b)
+            gelu_slab(0, 0, 0, 2 * b + 1)
+        start_pair(2)
         load_q.wait()
         qt = qt_v[...]
         q_all = stacked(split3(qt) + (jnp.zeros_like(qt),))
         for b in range(2 * N_CHUNK):
             q3_v[b] = q_all[:, b * LANES:(b + 1) * LANES]
-        step(0, 0, True, True, False, False)
-        start(AHEAD + 1)
-        step(1, 1, True, True, True, False)
+        step(0, 0, 0, True, True, False, False)
+        load_e(3).start()
+        load_e(4).start()
+        step(1, 0, 1, True, True, True, False)
 
         def pair(i, carry):
+            @pl.when(i + 2 < PAIRS)
+            def _():
+                start_pair(i + 2)
+
+            @pl.when(2 * i + 4 < N_CHUNK)
+            def _():
+                load_e(2 * i + 3).start()
+                load_e(2 * i + 4).start()
+
             for par in range(2):
                 c = 2 * i + par
 
-                @pl.when(c + AHEAD < N_CHUNK)
-                def _():
-                    start(c + AHEAD)
-
                 @pl.when(c + 1 < N_CHUNK)
                 def _():
-                    step(c, par, True, True, True, True)
+                    step(c, i, par, True, True, True, True)
             return carry
 
         lax.fori_loop(1, N_CHUNK // 2, pair, 0)
-        step(N_CHUNK - 1, 0, False, True, True, True)
-        step(N_CHUNK, 1, False, False, True, True)
-        step(N_CHUNK + 1, 0, False, False, False, True)
+        step(N_CHUNK - 1, 0, 0, False, True, True, True)
+        step(N_CHUNK, 0, 1, False, False, True, True)
+        step(N_CHUNK + 1, 0, 0, False, False, False, True)
         skip = 2 * CHUNK - SIDE
         out = []
         for q in range(2):
@@ -370,8 +392,10 @@
         out_specs=(vm, vm),
         scratch_shapes=[
             pltpu.VMEM((ROWS, D_IN), BF16),
-            pltpu.VMEM((N_CHUNK, ROWS, CHUNK), BF16),
-            pltpu.VMEM((N_CHUNK, ROWS, CHUNK), BF16),
+            pltpu.VMEM((ROWS, CHUNK), BF16),
+            pltpu.VMEM((ROWS, CHUNK), BF16),
+            pltpu.VMEM((PAIRS, ROWS, 2 * CHUNK), BF16),
+            pltpu.VMEM((PAIRS, ROWS, 2 * CHUNK), BF16),
             pltpu.VMEM((RANK, D_OUT), F32),
             pltpu.VMEM((ROWS // LANES, D_IN, LANES), BF16),
             pltpu.VMEM((2 * N_CHUNK, PADDED, LANES), BF16),
@@ -379,7 +403,8 @@
             pltpu.VMEM((2, ROWS, LANES), BF16),
             pltpu.VMEM((3, 2, D_IN, LANES), BF16),
             pltpu.VMEM((3, 2, D_IN, LANES), BF16),
-            pltpu.SemaphoreType.DMA((3, N_CHUNK)),
+            pltpu.SemaphoreType.DMA((N_CHUNK,)),
+            pltpu.SemaphoreType.DMA((2, PAIRS + 1)),
             pltpu.SemaphoreType.DMA,
             pltpu.SemaphoreType.DMA,
         ],

time: 55.3 us -> 54 us (0.976)
  Pallas kernels: 54.4 us -> 53.1 us
    pallas_call x1, Pallas kernels: 27 us -> 26.2 us  [per_device(): pl.pallas_call(merge_kernel, out_shape=(pltpu.VMEM((N_CHUNK, D_IN, CHUNK)...]
where the time goes in v8:
time: 54 us; the launch traced here: 53.9 us
  Pallas kernels  53.1 us (98%)
  between operations  0.81 us (2%)
    pallas_call x1, Pallas kernels, per_device(): pl.pallas_call(merge_kernel, out_shape=(pltpu.VMEM((N_CHUNK, D_IN, CHUNK)...  26.2 us
    pallas_call x1, Pallas kernels, per_device(): pl.pallas_call(factor_kernel, out_shape=(pltpu.VMEM((RANK, D_IN), F32), p...  20.4 us
    pallas_call x1, Pallas kernels, per_device(): pl.pallas_call(error_kernel, out_shape=(jax.ShapeDtypeStruct((D_IN, D_OUT...  6.53 us

profile of v8, /device:TPU:0, one launch (start us, length us, event | category | flops | bytes accessed | tf_op | source)
XLA Modules:
  0.0 53.9 jit_solution(11729037846566635514)
XLA Ops:
  0.6 26.2 %merge.1 = (f32[19,896,256]{2,1,0:T(8,128)S(1)}, f32[8,896]{1,0:T(8,128)S(1)}) custom-call(bf16[1024,896]{1,0:T(8,128)(2,1)} %a_hbm.1, bf16[1024,4864]{1,0:T(8,128)(2,1)} %z_hbm.1, bf16[1024,4864]{1,0:T(8,128)(2,1)} %dy_hbm.1, f32[8,4864]{1,0:T(8,128)} %bitcast.6, f32[896,4864]{1,0:T(8,128)} %bitcast.5), custom_call_target="tpu_custom_call" | custom-call | tf_op jit(solution)/shard_map/merge/pallas_call | solution.py:388
  26.8 20.4 %factor.1 = (f32[8,896]{1,0:T(8,128)S(1)}, f32[8,4864]{1,0:T(8,128)S(1)}, f32[19,896,256]{2,1,0:T(8,128)S(1)}) custom-call(f32[8,896]{1,0:T(8,128)S(1)} %get-tuple-element.11.p_in, f32[19,896,256]{2,1,0:T(8,128)S(1)} %get-tuple-element.12.m_in), custom_call_target="tpu_custom_call", output_to_operand_aliasing={{0}: (0, {}), {2}: (1, {})} | custom-call | tf_op jit(solution)/shard_map/factor/pallas_call | solution.py:414
  47.2 6.5 %new_error.1 = (f32[896,4864]{1,0:T(8,128)}, f32[8,896]{1,0:T(8,128)}, f32[8,4864]{1,0:T(8,128)}) custom-call(f32[8,896]{1,0:T(8,128)S(1)} %get-tuple-element.13.pt_ref, f32[8,4864]{1,0:T(8,128)S(1)} %get-tuple-element.14.qn_ref, f32[19,896,256]{2,1,0:T(8,128)S(1)} %get-tuple-element.15.m_ref), custom_call_target="tpu_custom_call" | custom-call | tf_op jit(solution)/shard_map/new_error/pallas_call | solution.py:441
